TPU v7x, 256 devices: a whole 4x4x8 slice. The times are simulated.
256 devices in a mesh: grp: 8 (over y, x_lo), tp: 32 (over z, x_hi, core).
Axes of the slice: x: 4 (x_hi: 2, x_lo: 2; x = x_hi * 2 + x_lo), y: 4, z: 8, core: 2. Of those that a mesh axis runs over, the one named last changes fastest.
Arguments:
- teacher_in: bfloat16 [384, 8192], P('tp', 'grp'), may hold values from -6 to 6
- teacher_gate: bfloat16 [8192, 28672], P('grp', 'tp'), may hold values from -0.0625 to 0.0625
- teacher_up: bfloat16 [8192, 28672], P('grp', 'tp'), may hold values from -0.0625 to 0.0625
- teacher_down: bfloat16 [28672, 8192], P('tp', 'grp'), may hold values from -0.0625 to 0.0625
- student_in: bfloat16 [384, 4096], P('tp', 'grp'), may hold values from -6 to 6
- student_gate: bfloat16 [4096, 14336], P('grp', 'tp'), may hold values from -0.09375 to 0.09375
- student_up: bfloat16 [4096, 14336], P('grp', 'tp'), may hold values from -0.09375 to 0.09375
- student_down: bfloat16 [14336, 4096], P('tp', 'grp'), may hold values from -0.046875 to 0.046875
- projector: bfloat16 [4096, 8, 1024], P('grp', None, 'tp'), may hold values from -0.09375 to 0.09375
Outputs:
- grad_input: float32 [384, 4096], P('tp', 'grp')
- grad_gate: float32 [4096, 14336], P('grp', 'tp')
- grad_up: float32 [4096, 14336], P('grp', 'tp')
- grad_down: float32 [14336, 4096], P('tp', 'grp')
- grad_projector: float32 [4096, 8, 1024], P('grp', None, 'tp')
All inputs are finite; a program needn't handle non-finite values.
Results may differ from a plain program's by a relative error of at most 0.017.
Values may be sent and summed in bfloat16 or wider, within the bound.
A program may use at most 64 MiB of HBM per device.

v0:
```python
import jax
import jax.numpy as jnp
from jax import lax
from jax.sharding import Mesh
from jax.sharding import PartitionSpec as P

TP = ("tp_0", "tp_1", "tp_2")


def laid_out(pieces, dim):
    dims = list(pieces.shape[1:])
    dims[dim] *= pieces.shape[0]
    return jnp.moveaxis(pieces, 0, dim).reshape(dims)


def copy_for_each(shard, axis):
    copies = jnp.broadcast_to(shard, (lax.axis_size(axis), *shard.shape))
    return lax.all_to_all(copies, axis, split_axis=0, concat_axis=0, tiled=True)


def gather_directly(shard, axis, dim):
    return laid_out(copy_for_each(shard, axis), dim)


def in_blocks(shard, dim, size):
    dims = shard.shape
    pieces = shard.reshape(*dims[:dim], size, dims[dim] // size, *dims[dim + 1 :])
    return jnp.moveaxis(pieces, dim, 0)


def sum_at_owner(shard, axis, dim):
    size = lax.axis_size(axis)
    pieces = lax.all_to_all(in_blocks(shard, dim, size), axis, 0, 0, tiled=True)
    return jnp.sum(pieces.astype(jnp.float32), axis=0)


def sum_at_owner_2(shard, axis, dim):
    pieces = in_blocks(shard, dim, lax.axis_size(axis))
    arrived = lax.all_to_all(pieces, axis, split_axis=0, concat_axis=0, tiled=True)
    return arrived.sum(axis=0)


def sum_in_two_steps(shard, axes, dim):
    far, near = axes
    pieces = in_blocks(shard, dim, lax.axis_size(far))
    nearer = sum_at_owner_2(pieces, near, dim + 1)
    arrived = lax.all_to_all(nearer, far, split_axis=0, concat_axis=0, tiled=True)
    return arrived.sum(axis=0)


def rows_for(lines, size):
    spare = -lines.shape[0] % size
    if not spare:
        return lines
    return jnp.concatenate([lines, jnp.zeros((spare, *lines.shape[1:]), lines.dtype)])


def gathered_by_axis(shard, axes, dim):
    far, near = axes
    initial = copy_for_each(shard, far)
    pieces = jnp.swapaxes(copy_for_each(initial, near), 0, 1)
    return laid_out(pieces.reshape(-1, *shard.shape), dim)


def nested_sum(shard, axes):
    lines = shard.reshape(-1, shard.shape[-1])
    own = sum_in_two_steps(
        rows_for(lines, lax.axis_size(axes[0]) * lax.axis_size(axes[1])), axes, 0
    )
    whole = gathered_by_axis(own, axes, 0)
    return whole[: len(lines)].reshape(shard.shape)


def body(
    teacher_in,
    teacher_gate,
    teacher_up,
    teacher_down,
    student_in,
    student_gate,
    student_up,
    student_down,
    projector,
):
    bf = jnp.bfloat16
    fl = jnp.float32
    teacher_pair = jnp.concatenate([teacher_gate, teacher_up], axis=1)
    teacher_width = teacher_gate.shape[1]
    teacher_partial = jnp.dot(
        gather_directly(teacher_in, TP, 0), teacher_pair, preferred_element_type=fl
    )
    teacher_pre = sum_at_owner(teacher_partial.astype(jnp.bfloat16), "grp", 0)
    teacher_hidden = (
        jax.nn.silu(teacher_pre[:, :teacher_width]) * teacher_pre[:, teacher_width:]
    ).astype(bf)
    teacher_sums = jnp.dot(
        gather_directly(teacher_hidden, "grp", 0), teacher_down, preferred_element_type=fl
    )
    teacher_share = sum_at_owner(teacher_sums.astype(jnp.bfloat16), TP, 1)
    teacher_feature = lax.all_to_all(
        teacher_share.astype(bf), "grp", split_axis=0, concat_axis=1, tiled=True
    )
    student_pair = jnp.concatenate([student_gate, student_up], axis=1)
    student_width = student_gate.shape[1]
    input_rows = gather_directly(student_in, TP, 0)
    student_partial = jnp.dot(input_rows, student_pair, preferred_element_type=fl)
    student_pre = sum_at_owner_2(student_partial, "grp", 0)
    gate_values = student_pre[:, :student_width]
    up_values = student_pre[:, student_width:]
    student_hidden = (jax.nn.silu(gate_values) * up_values).astype(bf)
    hidden_rows = gather_directly(student_hidden, "grp", 0)
    feature_sum = nested_sum(
        jnp.dot(hidden_rows, student_down, preferred_element_type=fl), (("tp_0", "tp_1"), "tp_2")
    )
    student_feature = feature_sum.astype(bf)
    proj_matrix = projector.reshape(projector.shape[0], -1)
    projected = sum_at_owner_2(
        jnp.dot(student_feature, proj_matrix, preferred_element_type=fl), "grp", 0
    )
    residual_grad = (projected - teacher_feature.astype(fl)).astype(bf)
    residual_rows = gather_directly(residual_grad, "grp", 0)
    grad_projector = jnp.dot(student_feature.T, residual_rows, preferred_element_type=fl).reshape(
        projector.shape
    )
    feature_grad = nested_sum(
        jnp.dot(residual_rows, proj_matrix.T, preferred_element_type=fl), (("tp_0", "tp_1"), "tp_2")
    ).astype(bf)
    grad_down = jnp.dot(hidden_rows.T, feature_grad, preferred_element_type=fl)
    hidden_grad = sum_at_owner_2(
        jnp.dot(feature_grad, student_down.T, preferred_element_type=fl), "grp", 0
    )
    sigmoid_gate = jax.nn.sigmoid(gate_values)
    gate_grad = (
        hidden_grad * up_values * sigmoid_gate * (1.0 + gate_values * (1.0 - sigmoid_gate))
    ).astype(bf)
    up_grad = (hidden_grad * gate_values * sigmoid_gate).astype(bf)
    pair_rows = gather_directly(jnp.concatenate([gate_grad, up_grad], axis=1), "grp", 0)
    grad_pair = jnp.dot(input_rows.T, pair_rows, preferred_element_type=fl)
    grad_input = sum_at_owner(
        jnp.dot(pair_rows, student_pair.T, preferred_element_type=fl).astype(jnp.bfloat16), TP, 0
    )
    return (
        grad_input,
        grad_pair[:, :student_width],
        grad_pair[:, student_width:],
        grad_down,
        grad_projector,
    )


def solution(mesh):
    torus = Mesh(mesh.devices.reshape(mesh.shape["grp"], 8, 2, 2), ("grp", "tp_0", "tp_1", "tp_2"))
    in_specs = (
        P(TP, "grp"),
        P("grp", TP),
        P("grp", TP),
        P(TP, "grp"),
        P(TP, "grp"),
        P("grp", TP),
        P("grp", TP),
        P(TP, "grp"),
        P("grp", None, TP),
    )
    out_specs = (P(TP, "grp"), P("grp", TP), P("grp", TP), P(TP, "grp"), P("grp", None, TP))
    return jax.shard_map(body, mesh=torus, in_specs=in_specs, out_specs=out_specs, check_vma=False)
```

profile of v0, /device:TPU:53, one launch (start us, length us, event | category | flops | bytes accessed | tf_op | source)
XLA Modules:
  0.0 364.3 jit_solution(10201312632511793941)
XLA Ops:
  1.6 27.7 %all_to_all.113 = bf16[32,12,512]{2,1,0:T(8,128)(2,1)} all-to-all(bf16[32,12,512]{2,1,0:T(8,128)(2,1)S(1)} %broadcast_in_dim.30), channel_id=1, replica_groups=mesh['grp'=8,'tp_0'=8,'tp_1'=2,'tp_2'=2] {'tp_0','tp_1','tp_2'}, dimensions={0} | all-to-all | bytes 786432 | tf_op jit(solution)/shard_map/all_to_all | solution.py:18
  31.2 6.3 %all-to-all-start.8 = ((bf16[32,12,1024]{2,1,0:T(8,128)(2,1)}), bf16[32,12,1024]{2,1,0:T(8,128)(2,1)S(1)}, u32[]{:S(2)}, u32[]{:S(2)}) async-start(bf16[32,12,1024]{2,1,0:T(8,128)(2,1)} %broadcast_in_dim.34), calls=%async_computation.8 | async-start | bytes 2097152 | tf_op jit(solution)/shard_map/all_to_all | solution.py:18
  44.3 21.1 %all-to-all-done.8 = bf16[32,12,1024]{2,1,0:T(8,128)(2,1)S(1)} async-done(((bf16[32,12,1024]{2,1,0:T(8,128)(2,1)}), bf16[32,12,1024]{2,1,0:T(8,128)(2,1)S(1)}, u32[]{:S(2)}, u32[]{:S(2)}) %all-to-all-start.8) | async-done | bytes 786464 | tf_op jit(solution)/shard_map/all_to_all | solution.py:18
  66.3 4.9 %all-to-all-start.1 = ((f32[8,48,896]{2,1,0:T(8,128)}), f32[8,48,896]{2,1,0:T(8,128)S(1)}, u32[]{:S(2)}, u32[]{:S(2)}) async-start(f32[8,48,896]{2,1,0:T(8,128)} %bitcast.68), calls=%async_computation.1 | async-start | bytes 2752512 | tf_op jit(solution)/shard_map/all_to_all | solution.py:39
  73.3 14.0 %all-to-all-done.1 = f32[8,48,896]{2,1,0:T(8,128)S(1)} async-done(((f32[8,48,896]{2,1,0:T(8,128)}), f32[8,48,896]{2,1,0:T(8,128)S(1)}, u32[]{:S(2)}, u32[]{:S(2)}) %all-to-all-start.1) | async-done | bytes 1376288 | tf_op jit(solution)/shard_map/all_to_all | solution.py:39
  88.3 6.0 %all-to-all-start.2 = ((bf16[8,48,448]{2,1,0:T(8,128)(2,1)}), bf16[8,48,448]{2,1,0:T(8,128)(2,1)S(1)}, u32[]{:S(2)}, u32[]{:S(2)}) async-start(bf16[8,48,448]{2,1,0:T(8,128)(2,1)} %broadcast_in_dim.31), calls=%async_computation.2 | async-start | bytes 786432 | tf_op jit(solution)/shard_map/all_to_all | solution.py:18
  94.3 5.0 %fusion.4 = bf16[1792,384]{0,1:T(8,128)(2,1)} fusion(bf16[384,1024]{1,0:T(8,128)(2,1)} %reshape.67, bf16[1024,896]{1,0:T(8,128)(2,1)} %param.11, bf16[1024,896]{1,0:T(8,128)(2,1)} %param.10), kind=kOutput, calls=%fused_computation.4 | convolution fusion | flops 1417314304 | bytes 5832704 | tf_op jit(solution)/shard_map/dot_general | solution.py:89
  99.9 7.0 %all_to_all.114 = f32[2,16,12,512]{3,1,2,0:T(8,128)} all-to-all(f32[2,16,12,512]{3,1,2,0:T(8,128)S(1)} %convolution_bitcast_fusion.1), channel_id=1, replica_groups=mesh['grp'=8,'tp_0'=8,'tp_1'=2,'tp_2'=2] {'tp_2'}, dimensions={0} | all-to-all | bytes 1572864 | tf_op jit(solution)/shard_map/all_to_all | solution.py:39
  106.9 5.8 %all-to-all-start.9 = ((bf16[8,48,1792]{2,1,0:T(8,128)(2,1)}), bf16[8,48,1792]{2,1,0:T(8,128)(2,1)S(1)}, u32[]{:S(2)}, u32[]{:S(2)}) async-start(bf16[8,48,1792]{2,1,0:T(8,128)(2,1)} %bitcast.73), calls=%async_computation.9 | async-start | bytes 2752512 | tf_op jit(solution)/shard_map/all_to_all | solution.py:33
  116.7 12.6 %all-to-all-done.9 = bf16[8,48,1792]{2,1,0:T(8,128)(2,1)S(1)} async-done(((bf16[8,48,1792]{2,1,0:T(8,128)(2,1)}), bf16[8,48,1792]{2,1,0:T(8,128)(2,1)S(1)}, u32[]{:S(2)}, u32[]{:S(2)}) %all-to-all-start.9) | async-done | bytes 1376288 | tf_op jit(solution)/shard_map/all_to_all | solution.py:33
  129.3 5.2 %all-to-all-start.4 = ((f32[16,12,512]{2,1,0:T(8,128)}), f32[16,12,512]{2,1,0:T(8,128)}, u32[]{:S(2)}, u32[]{:S(2)}) async-start(f32[16,12,512]{2,1,0:T(8,128)} %copy.42), calls=%async_computation.4 | async-start | bytes 1048576 | tf_op jit(solution)/shard_map/all_to_all | solution.py:47
  134.7 12.2 %all-to-all-done.4 = f32[16,12,512]{2,1,0:T(8,128)} async-done(((f32[16,12,512]{2,1,0:T(8,128)}), f32[16,12,512]{2,1,0:T(8,128)}, u32[]{:S(2)}, u32[]{:S(2)}) %all-to-all-start.4) | async-done | bytes 393248 | tf_op jit(solution)/shard_map/all_to_all | solution.py:47
  147.8 7.4 %all-to-all-start.10 = ((bf16[8,48,896]{2,1,0:T(8,128)(2,1)}), bf16[8,48,896]{2,1,0:T(8,128)(2,1)S(1)}, u32[]{:S(2)}, u32[]{:S(2)}) async-start(bf16[8,48,896]{2,1,0:T(8,128)(2,1)} %broadcast_in_dim.35), calls=%async_computation.10 | async-start | bytes 1376256 | tf_op jit(solution)/shard_map/all_to_all | solution.py:18
  156.2 6.5 %all-to-all-done.10 = bf16[8,48,896]{2,1,0:T(8,128)(2,1)S(1)} async-done(((bf16[8,48,896]{2,1,0:T(8,128)(2,1)}), bf16[8,48,896]{2,1,0:T(8,128)(2,1)S(1)}, u32[]{:S(2)}, u32[]{:S(2)}) %all-to-all-start.10) | async-done | bytes 688160 | tf_op jit(solution)/shard_map/all_to_all | solution.py:18
  163.6 9.2 %all-to-all-start.5 = ((bf16[16,12,512]{2,1,0:T(8,128)(2,1)}), bf16[16,12,512]{2,1,0:T(8,128)(2,1)S(1)}, u32[]{:S(2)}, u32[]{:S(2)}) async-start(bf16[16,12,512]{2,1,0:T(8,128)(2,1)} %broadcast_in_dim.32), calls=%async_computation.5 | async-start | bytes 524288 | tf_op jit(solution)/shard_map/all_to_all | solution.py:18
  176.1 4.4 %all-to-all-done.5 = bf16[16,12,512]{2,1,0:T(8,128)(2,1)S(1)} async-done(((bf16[16,12,512]{2,1,0:T(8,128)(2,1)}), bf16[16,12,512]{2,1,0:T(8,128)(2,1)S(1)}, u32[]{:S(2)}, u32[]{:S(2)}) %all-to-all-start.5) | async-done | bytes 196640 | tf_op jit(solution)/shard_map/all_to_all | solution.py:18
  180.6 7.6 %all_to_all.115 = bf16[2,16,12,512]{3,1,2,0:T(8,128)(2,1)} all-to-all(bf16[2,16,12,512]{3,1,2,0:T(8,128)(2,1)S(1)} %broadcast_in_dim.33), channel_id=1, replica_groups=mesh['grp'=8,'tp_0'=8,'tp_1'=2,'tp_2'=2] {'tp_2'}, dimensions={0} | all-to-all | bytes 786432 | tf_op jit(solution)/shard_map/all_to_all | solution.py:18
  188.2 7.7 %all-to-all-start.11 = ((bf16[32,384,32]{1,2,0:T(8,128)(2,1)}), bf16[32,384,32]{1,2,0:T(8,128)(2,1)S(1)}, u32[]{:S(2)}, u32[]{:S(2)}) async-start(bf16[32,384,32]{1,2,0:T(8,128)(2,1)} %bitcast.12), calls=%async_computation.11 | async-start | bytes 1572864 | tf_op jit(solution)/shard_map/all_to_all | solution.py:33
  200.1 17.5 %all-to-all-done.11 = bf16[32,384,32]{1,2,0:T(8,128)(2,1)S(1)} async-done(((bf16[32,384,32]{1,2,0:T(8,128)(2,1)}), bf16[32,384,32]{1,2,0:T(8,128)(2,1)S(1)}, u32[]{:S(2)}, u32[]{:S(2)}) %all-to-all-start.11) | async-done | bytes 786464 | tf_op jit(solution)/shard_map/all_to_all | solution.py:33
  217.6 6.1 %all-to-all-start.7 = ((f32[8,48,256]{2,1,0:T(8,128)}), f32[8,48,256]{2,1,0:T(8,128)}, u32[]{:S(2)}, u32[]{:S(2)}) async-start(f32[8,48,256]{2,1,0:T(8,128)} %fusion.16), calls=%async_computation.7 | async-start | bytes 786432 | tf_op jit(solution)/shard_map/all_to_all | solution.py:39
  224.8 4.0 %all-to-all-done.7 = f32[8,48,256]{2,1,0:T(8,128)} async-done(((f32[8,48,256]{2,1,0:T(8,128)}), f32[8,48,256]{2,1,0:T(8,128)}, u32[]{:S(2)}, u32[]{:S(2)}) %all-to-all-start.7) | async-done | bytes 393248 | tf_op jit(solution)/shard_map/all_to_all | solution.py:39
  228.8 5.9 %all-to-all-start.12 = ((bf16[8,2,768]{2,1,0:T(2,128)(2,1)}), bf16[8,2,768]{2,1,0:T(2,128)(2,1)S(1)}, u32[]{:S(2)}, u32[]{:S(2)}) async-start(bf16[8,2,768]{2,1,0:T(2,128)(2,1)} %reshape.82), calls=%async_computation.12 | async-start | bytes 49152 | tf_op jit(solution)/shard_map/all_to_all | solution.py:100
  238.0 8.2 %all_to_all.116 = bf16[8,48,256]{2,1,0:T(8,128)(2,1)S(1)} all-to-all(bf16[8,48,256]{2,1,0:T(8,128)(2,1)S(1)} %broadcast_in_dim.36), channel_id=1, replica_groups=mesh['grp'=8,'tp_0'=8,'tp_1'=2,'tp_2'=2] {'grp'}, dimensions={0} | all-to-all | bytes 393216 | tf_op jit(solution)/shard_map/all_to_all | solution.py:18
  247.1 8.4 %all_to_all.117 = f32[2,16,12,512]{3,1,2,0:T(8,128)S(1)} all-to-all(f32[2,16,12,512]{3,1,2,0:T(8,128)S(1)} %convolution_bitcast_fusion.2), channel_id=1, replica_groups=mesh['grp'=8,'tp_0'=8,'tp_1'=2,'tp_2'=2] {'tp_2'}, dimensions={0} | all-to-all | bytes 1572864 | tf_op jit(solution)/shard_map/all_to_all | solution.py:39
  257.5 19.5 %all_to_all.118 = f32[16,12,512]{2,1,0:T(8,128)S(1)} all-to-all(f32[16,12,512]{2,1,0:T(8,128)S(1)} %copy.51), channel_id=1, replica_groups=mesh['grp'=8,'tp_0'=8,'tp_1'=2,'tp_2'=2] {'tp_0','tp_1'}, dimensions={0} | all-to-all | bytes 786432 | tf_op jit(solution)/shard_map/all_to_all | solution.py:47
  277.1 16.2 %all_to_all.119 = bf16[16,12,512]{2,1,0:T(8,128)(2,1)S(1)} all-to-all(bf16[16,12,512]{2,1,0:T(8,128)(2,1)S(1)} %broadcast_in_dim.37), channel_id=1, replica_groups=mesh['grp'=8,'tp_0'=8,'tp_1'=2,'tp_2'=2] {'tp_0','tp_1'}, dimensions={0} | all-to-all | bytes 393216 | tf_op jit(solution)/shard_map/all_to_all | solution.py:18
  293.4 6.3 %all_to_all.120 = bf16[2,16,12,512]{3,1,2,0:T(8,128)(2,1)S(1)} all-to-all(bf16[2,16,12,512]{3,1,2,0:T(8,128)(2,1)S(1)} %broadcast_in_dim.38), channel_id=1, replica_groups=mesh['grp'=8,'tp_0'=8,'tp_1'=2,'tp_2'=2] {'tp_2'}, dimensions={0} | all-to-all | bytes 786432 | tf_op jit(solution)/shard_map/all_to_all | solution.py:18
  302.3 15.4 %all_to_all.121 = f32[8,48,448]{2,1,0:T(8,128)} all-to-all(f32[8,48,448]{2,1,0:T(8,128)S(1)} %fusion.8), channel_id=1, replica_groups=mesh['grp'=8,'tp_0'=8,'tp_1'=2,'tp_2'=2] {'grp'}, dimensions={0} | all-to-all | bytes 1376256 | tf_op jit(solution)/shard_map/all_to_all | solution.py:39
  320.0 6.5 %all-to-all-start.19 = ((bf16[8,48,896]{2,1,0:T(8,128)(2,1)}), bf16[8,48,896]{2,1,0:T(8,128)(2,1)}, u32[]{:S(2)}, u32[]{:S(2)}) async-start(bf16[8,48,896]{2,1,0:T(8,128)(2,1)} %broadcast_in_dim.39), calls=%async_computation.19 | async-start | bytes 1376256 | tf_op jit(solution)/shard_map/all_to_all | solution.py:18
  328.0 6.7 %all-to-all-done.19 = bf16[8,48,896]{2,1,0:T(8,128)(2,1)} async-done(((bf16[8,48,896]{2,1,0:T(8,128)(2,1)}), bf16[8,48,896]{2,1,0:T(8,128)(2,1)}, u32[]{:S(2)}, u32[]{:S(2)}) %all-to-all-start.19) | async-done | bytes 688160 | tf_op jit(solution)/shard_map/all_to_all | solution.py:18
  337.6 9.5 %all-to-all-start.20 = ((bf16[32,12,512]{2,1,0:T(8,128)(2,1)}), bf16[32,12,512]{2,1,0:T(8,128)(2,1)S(1)}, u32[]{:S(2)}, u32[]{:S(2)}) async-start(bf16[32,12,512]{2,1,0:T(8,128)(2,1)} %reshape.72), calls=%async_computation.20 | async-start | bytes 1048576 | tf_op jit(solution)/shard_map/all_to_all | solution.py:33
  351.6 12.0 %all-to-all-done.20 = bf16[32,12,512]{2,1,0:T(8,128)(2,1)S(1)} async-done(((bf16[32,12,512]{2,1,0:T(8,128)(2,1)}), bf16[32,12,512]{2,1,0:T(8,128)(2,1)S(1)}, u32[]{:S(2)}, u32[]{:S(2)}) %all-to-all-start.20) | async-done | bytes 393248 | tf_op jit(solution)/shard_map/all_to_all | solution.py:33
  (87 shorter events, 50.5 us)
Async XLA Ops:
  0.6 172.2 %copy-start = (bf16[896,1024]{1,0:T(8,128)(2,1)S(1)}, bf16[896,1024]{1,0:T(8,128)(2,1)}, u32[]{:S(2)}) copy-start(bf16[896,1024]{1,0:T(8,128)(2,1)} %param.12) | copy-start | bytes 5505028
  29.2 8.2 %copy-start.11 = (bf16[512,448]{0,1:T(8,128)(2,1)S(1)}, bf16[512,448]{0,1:T(8,128)(2,1)}, u32[]{:S(2)}) copy-start(bf16[512,448]{0,1:T(8,128)(2,1)} %param.14) | copy-start | bytes 1376260
  31.2 34.2 %all-to-all-start.8 = ((bf16[32,12,1024]{2,1,0:T(8,128)(2,1)}), bf16[32,12,1024]{2,1,0:T(8,128)(2,1)S(1)}, u32[]{:S(2)}, u32[]{:S(2)}) async-start(bf16[32,12,1024]{2,1,0:T(8,128)(2,1)} %broadcast_in_dim.34), calls=%async_computation.8 | async-start | bytes 2097152 | tf_op jit(solution)/shard_map/all_to_all | solution.py:18
  41.2 24.1 %copy-start.4 = (bf16[384,512]{1,0:T(8,128)(2,1)}, bf16[384,512]{1,0:T(8,128)(2,1)S(1)}, u32[]{:S(2)}) copy-start(bf16[384,512]{1,0:T(8,128)(2,1)S(1)} %reshape.64) | copy-start | bytes 1179652
  65.3 1.0 copy-start.1
  66.3 21.0 %all-to-all-start.1 = ((f32[8,48,896]{2,1,0:T(8,128)}), f32[8,48,896]{2,1,0:T(8,128)S(1)}, u32[]{:S(2)}, u32[]{:S(2)}) async-start(f32[8,48,896]{2,1,0:T(8,128)} %bitcast.68), calls=%async_computation.1 | async-start | bytes 2752512 | tf_op jit(solution)/shard_map/all_to_all | solution.py:39
  88.3 11.1 %all-to-all-start.2 = ((bf16[8,48,448]{2,1,0:T(8,128)(2,1)}), bf16[8,48,448]{2,1,0:T(8,128)(2,1)S(1)}, u32[]{:S(2)}, u32[]{:S(2)}) async-start(bf16[8,48,448]{2,1,0:T(8,128)(2,1)} %broadcast_in_dim.31), calls=%async_computation.2 | async-start | bytes 786432 | tf_op jit(solution)/shard_map/all_to_all | solution.py:18
  94.3 5.2 %copy-start.6 = (bf16[448,512]{1,0:T(8,128)(2,1)S(1)}, bf16[448,512]{1,0:T(8,128)(2,1)}, u32[]{:S(2)}) copy-start(bf16[448,512]{1,0:T(8,128)(2,1)} %param.16) | copy-start | bytes 1376260
  99.3 7.5 %copy-start.2 = (bf16[8,48,448]{2,1,0:T(8,128)(2,1)}, bf16[8,48,448]{2,1,0:T(8,128)(2,1)S(1)}, u32[]{:S(2)}) copy-start(bf16[8,48,448]{2,1,0:T(8,128)(2,1)S(1)} %all-to-all-done.2) | copy-start | bytes 1032196
  106.9 22.4 %all-to-all-start.9 = ((bf16[8,48,1792]{2,1,0:T(8,128)(2,1)}), bf16[8,48,1792]{2,1,0:T(8,128)(2,1)S(1)}, u32[]{:S(2)}, u32[]{:S(2)}) async-start(bf16[8,48,1792]{2,1,0:T(8,128)(2,1)} %bitcast.73), calls=%async_computation.9 | async-start | bytes 2752512 | tf_op jit(solution)/shard_map/all_to_all | solution.py:33
  129.3 17.6 %all-to-all-start.4 = ((f32[16,12,512]{2,1,0:T(8,128)}), f32[16,12,512]{2,1,0:T(8,128)}, u32[]{:S(2)}, u32[]{:S(2)}) async-start(f32[16,12,512]{2,1,0:T(8,128)} %copy.42), calls=%async_computation.4 | async-start | bytes 1048576 | tf_op jit(solution)/shard_map/all_to_all | solution.py:47
  147.8 15.0 %all-to-all-start.10 = ((bf16[8,48,896]{2,1,0:T(8,128)(2,1)}), bf16[8,48,896]{2,1,0:T(8,128)(2,1)S(1)}, u32[]{:S(2)}, u32[]{:S(2)}) async-start(bf16[8,48,896]{2,1,0:T(8,128)(2,1)} %broadcast_in_dim.35), calls=%async_computation.10 | async-start | bytes 1376256 | tf_op jit(solution)/shard_map/all_to_all | solution.py:18
  162.8 10.0 %copy-start.10 = (bf16[8,48,896]{2,1,0:T(8,128)(2,1)}, bf16[8,48,896]{2,1,0:T(8,128)(2,1)S(1)}, u32[]{:S(2)}) copy-start(bf16[8,48,896]{2,1,0:T(8,128)(2,1)S(1)} %all-to-all-done.10) | copy-start | bytes 2064388
  163.6 16.9 %all-to-all-start.5 = ((bf16[16,12,512]{2,1,0:T(8,128)(2,1)}), bf16[16,12,512]{2,1,0:T(8,128)(2,1)S(1)}, u32[]{:S(2)}, u32[]{:S(2)}) async-start(bf16[16,12,512]{2,1,0:T(8,128)(2,1)} %broadcast_in_dim.32), calls=%async_computation.5 | async-start | bytes 524288 | tf_op jit(solution)/shard_map/all_to_all | solution.py:18
  188.2 29.4 %all-to-all-start.11 = ((bf16[32,384,32]{1,2,0:T(8,128)(2,1)}), bf16[32,384,32]{1,2,0:T(8,128)(2,1)S(1)}, u32[]{:S(2)}, u32[]{:S(2)}) async-start(bf16[32,384,32]{1,2,0:T(8,128)(2,1)} %bitcast.12), calls=%async_computation.11 | async-start | bytes 1572864 | tf_op jit(solution)/shard_map/all_to_all | solution.py:33
  217.6 11.2 %all-to-all-start.7 = ((f32[8,48,256]{2,1,0:T(8,128)}), f32[8,48,256]{2,1,0:T(8,128)}, u32[]{:S(2)}, u32[]{:S(2)}) async-start(f32[8,48,256]{2,1,0:T(8,128)} %fusion.16), calls=%async_computation.7 | async-start | bytes 786432 | tf_op jit(solution)/shard_map/all_to_all | solution.py:39
  223.9 23.0 %copy-start.9 = (bf16[512,8,32]{0,2,1:T(8,128)(2,1)S(1)}, bf16[512,8,32]{0,2,1:T(8,128)(2,1)}, u32[]{:S(2)}) copy-start(bf16[512,8,32]{0,2,1:T(8,128)(2,1)} %param.17) | copy-start | bytes 786436
  228.8 9.0 %all-to-all-start.12 = ((bf16[8,2,768]{2,1,0:T(2,128)(2,1)}), bf16[8,2,768]{2,1,0:T(2,128)(2,1)S(1)}, u32[]{:S(2)}, u32[]{:S(2)}) async-start(bf16[8,2,768]{2,1,0:T(2,128)(2,1)} %reshape.82), calls=%async_computation.12 | async-start | bytes 49152 | tf_op jit(solution)/shard_map/all_to_all | solution.py:100
  246.2 0.7 copy-start.7
  318.9 7.7 %copy-start.8 = (bf16[8,48,256]{2,1,0:T(8,128)(2,1)S(1)}, bf16[8,48,256]{2,1,0:T(8,128)(2,1)}, u32[]{:S(2)}) copy-start(bf16[8,48,256]{2,1,0:T(8,128)(2,1)} %copy-done.7) | copy-start | bytes 589828
  320.0 14.6 %all-to-all-start.19 = ((bf16[8,48,896]{2,1,0:T(8,128)(2,1)}), bf16[8,48,896]{2,1,0:T(8,128)(2,1)}, u32[]{:S(2)}, u32[]{:S(2)}) async-start(bf16[8,48,896]{2,1,0:T(8,128)(2,1)} %broadcast_in_dim.39), calls=%async_computation.19 | async-start | bytes 1376256 | tf_op jit(solution)/shard_map/all_to_all | solution.py:18
  334.7 12.4 %copy-start.3 = (bf16[8,48,448]{2,1,0:T(8,128)(2,1)S(1)}, bf16[8,48,448]{2,1,0:T(8,128)(2,1)}, u32[]{:S(2)}) copy-start(bf16[8,48,448]{2,1,0:T(8,128)(2,1)} %copy-done.2) | copy-start | bytes 1032196
  336.7 11.8 %copy-start.5 = (bf16[384,512]{1,0:T(8,128)(2,1)S(1)}, bf16[384,512]{1,0:T(8,128)(2,1)}, u32[]{:S(2)}) copy-start(bf16[384,512]{1,0:T(8,128)(2,1)} %copy-done.4) | copy-start | bytes 1179652
  337.6 26.1 %all-to-all-start.20 = ((bf16[32,12,512]{2,1,0:T(8,128)(2,1)}), bf16[32,12,512]{2,1,0:T(8,128)(2,1)S(1)}, u32[]{:S(2)}, u32[]{:S(2)}) async-start(bf16[32,12,512]{2,1,0:T(8,128)(2,1)} %reshape.72), calls=%async_computation.20 | async-start | bytes 1048576 | tf_op jit(solution)/shard_map/all_to_all | solution.py:33
where the time goes:
time: 371 us; the launch traced here: 364 us
  blocking collectives  116 us (31%)
  waiting for transfers between devices  113 us (30%)
  starting transfers between devices  80.5 us (22%)
  local copies, waits for them, and re-layouts  25.3 us (7%)
  matrix products  20.7 us (6%)
  other arithmetic  7.56 us (2%)
    all_to_all x5, blocking collectives, copy_for_each(): return lax.all_to_all(copies, axis, split_axis=0, concat_axis=0, tiled=True)  66 us
    all_to_all x3, waiting for transfers between devices, sum_at_owner(): pieces = lax.all_to_all(in_blocks(shard, dim, size), axis, 0, 0, tiled=True)  42.1 us
    all_to_all x5, waiting for transfers between devices, copy_for_each(): return lax.all_to_all(copies, axis, split_axis=0, concat_axis=0, tiled=True)  38.7 us
    all_to_all x5, starting transfers between devices, copy_for_each(): return lax.all_to_all(copies, axis, split_axis=0, concat_axis=0, tiled=True)  35.4 us
    all_to_all x3, blocking collectives, sum_at_owner_2(): lax.all_to_all(pieces, axis, split_axis=0, concat_axis=0, tiled=True)  30.8 us
    all_to_all x3, starting transfers between devices, sum_at_owner(): pieces = lax.all_to_all(in_blocks(shard, dim, size), axis, 0, 0, tiled=True)  23.1 us
    all_to_all x1, blocking collectives, sum_in_two_steps(): lax.all_to_all(nearer, far, split_axis=0, concat_axis=0, tiled=True)  19.5 us
    all_to_all x2, waiting for transfers between devices, sum_at_owner_2(): lax.all_to_all(pieces, axis, split_axis=0, concat_axis=0, tiled=True)  18.1 us
  transfers between devices with their start and end apart: 12, of which 11 were waited for; matrix products, arithmetic and copies ran while one was open for 9% of the time, Pallas kernels for 0%

commit v1 on v0

v1 whole, which is shorter than its diff:
```python
import functools

import jax
import jax.numpy as jnp
from jax import lax
from jax.experimental import pallas as pl
from jax.experimental.pallas import tpu as pltpu
from jax.sharding import Mesh
from jax.sharding import PartitionSpec as P

AXES = ("y", "xl", "z", "xh", "c")
TP = ("z", "xh", "c")
GRP = ("y", "xl")
BF = jnp.bfloat16
FL = jnp.float32


def dot(a, b, ca, cb):
    return lax.dot_general(a, b, (((ca,), (cb,)), ((), ())), preferred_element_type=FL)


def kernel(
    sizes,
    t_in, t_gate, t_up, t_down, s_in, s_gate, s_up, s_down, proj_t,
    o_x, o_h, o_f, o_rt, o_fg, o_gg, o_ug, o_gi,
    w_tg, w_tu, w_td, w_tdt, w_sp, w_sd, w_pt,
    xs, xtmp, x, s2s, s2r, pv, h,
    f_keep, f_cs, f_cr, f_rs, f_rr, f,
    p_s, p_r, rt,
    g_keep, g_cs, g_cr, g_rs, g_rr, fg,
    h_s, h_r, gu, gg, ug,
    gi_f, gi_cs, gi_cr, gi_rs, gi_rr, gi,
    ts, ttmp, tx, t2s, t2r, t2a, th,
    tf_keep, tf_cs, tf_cr, tf_rs, tf_rr, tf,
    w_sem, i_sem, o_sem, grp_ss, grp_rs, tp_ss, tp_rs, fw_ss, fw_rs, c_ss, c_rs,
):
    Y, XL, Z, XH = sizes
    G = Y * XL
    N = Z * XH
    y = lax.axis_index("y")
    xl = lax.axis_index("xl")
    z = lax.axis_index("z")
    xh = lax.axis_index("xh")
    c = lax.axis_index("c")
    o = 1 - c
    g = y * XL + xl
    RZ = x.shape[0] // Z
    RB = RZ // (2 * XH)

    def grp_to(k):
        return {"y": lax.rem(y + k // XL, Y), "xl": lax.rem(xl + lax.rem(k, XL), XL)}

    def grp_from(k):
        return lax.rem(y + Y - k // XL, Y) * XL + lax.rem(xl + XL - lax.rem(k, XL), XL)

    def tp_to(k):
        return {"z": lax.rem(z + k // XH, Z), "xh": lax.rem(xh + lax.rem(k, XH), XH)}

    def tp_from(k):
        return lax.rem(z + Z - k // XH, Z), lax.rem(xh + XH - lax.rem(k, XH), XH)

    other = {"c": o}

    def rdma(src, dst, ss, rs, dev):
        return pltpu.make_async_remote_copy(
            src_ref=src, dst_ref=dst, send_sem=ss, recv_sem=rs,
            device_id=dev, device_id_type=pl.DeviceIdType.MESH,
        )

    def loop(lo, hi, body):
        def step(i, carry):
            body(i)
            return carry

        lax.fori_loop(lo, hi, step, 0)

    late = []

    def grp_rs_copy(ph, k, send, recv):
        to = grp_to(k)
        return rdma(
            send.at[to["y"] * XL + to["xl"]], recv.at[k - 1],
            grp_ss.at[ph, k], grp_rs.at[ph, k], to,
        )

    def grp_rs_start(ph, send, recv):
        loop(1, G, lambda k: grp_rs_copy(ph, k, send, recv).start())
        late.append(lambda: loop(1, G, lambda k: grp_rs_copy(ph, k, send, recv).wait_send()))

    def grp_ag_copy(ph, k, buf, at):
        return rdma(buf.at[at(g)], buf.at[at(g)], grp_ss.at[ph, k], grp_rs.at[ph, k], grp_to(k))

    def grp_ag_start(ph, buf, at):
        loop(1, G, lambda k: grp_ag_copy(ph, k, buf, at).start())
        late.append(lambda: loop(1, G, lambda k: grp_ag_copy(ph, k, buf, at).wait_send()))

    def grp_ag_wait(ph, buf, at):
        def one(k):
            src = grp_from(k)
            rdma(
                buf.at[at(src)], buf.at[at(src)], grp_ss.at[ph, k], grp_rs.at[ph, k], grp_to(k)
            ).wait_recv()

        loop(1, G, one)

    def tp_ag_start(ph, buf, at):
        mine = buf.at[at(z, xh, c)]
        loop(1, N, lambda k: rdma(mine, mine, tp_ss.at[ph, k], tp_rs.at[ph, k], tp_to(k)).start())
        rdma(mine, mine, fw_ss.at[ph, 0], fw_rs.at[ph, 0], other).start()
        late.append(
            lambda: loop(
                1, N, lambda k: rdma(mine, mine, tp_ss.at[ph, k], tp_rs.at[ph, k], tp_to(k)).wait_send()
            )
        )
        late.append(
            lambda: loop(
                0, N, lambda k: rdma(mine, mine, fw_ss.at[ph, k], fw_rs.at[ph, k], other).wait_send()
            )
        )

    def tp_ag_forward(ph, buf, at):
        def one(k):
            zz, xx = tp_from(k)
            block = buf.at[at(zz, xx, c)]
            rdma(block, block, tp_ss.at[ph, k], tp_rs.at[ph, k], tp_to(k)).wait_recv()
            rdma(block, block, fw_ss.at[ph, k], fw_rs.at[ph, k], other).start()

        loop(1, N, one)

    def tp_ag_wait(ph, buf, at):
        def one(k):
            zz, xx = tp_from(k)
            block = buf.at[at(zz, xx, o)]
            rdma(block, block, fw_ss.at[ph, k], fw_rs.at[ph, k], other).wait_recv()

        loop(0, N, one)

    def c_copy(ph, src, dst):
        return rdma(src, dst, c_ss.at[ph], c_rs.at[ph], other)

    def c_start(ph, src, dst):
        c_copy(ph, src, dst).start()
        late.append(lambda: c_copy(ph, src, dst).wait_send())

    def tp_rs_copy(ph, k, send, recv):
        to = tp_to(k)
        return rdma(
            send.at[to["z"] * XH + to["xh"]], recv.at[k - 1], tp_ss.at[ph, k], tp_rs.at[ph, k], to
        )

    def tp_rs_start(ph, send, recv):
        loop(1, N, lambda k: tp_rs_copy(ph, k, send, recv).start())
        late.append(lambda: loop(1, N, lambda k: tp_rs_copy(ph, k, send, recv).wait_send()))

    def summed(n, copy, recv, first):
        def step(k, acc):
            copy(k).wait_recv()
            return acc + recv[k - 1].astype(FL)

        return lax.fori_loop(1, n, step, first)

    def tp_rs_sum(ph, send, recv):
        return summed(N, lambda k: tp_rs_copy(ph, k, send, recv), recv, send[z * XH + xh].astype(FL))

    def grp_rs_sum(ph, send, recv):
        return summed(G, lambda k: grp_rs_copy(ph, k, send, recv), recv, send[g].astype(FL))

    FS_L = s_gate.shape[0]
    A = FS_L // 128 * 128
    B = FS_L - A
    loads = [
        pltpu.make_async_copy(src, dst, w_sem.at[i])
        for i, (src, dst) in enumerate(
            (
                (s_gate.at[:A], w_sp.at[:A]), (s_up.at[:A], w_sp.at[A : 2 * A]),
                (s_gate.at[A:], w_sp.at[2 * A : A + FS_L]), (s_up.at[A:], w_sp.at[A + FS_L :]),
                (t_gate, w_tg), (t_up, w_tu), (t_down, w_td), (s_down, w_sd), (proj_t, w_pt),
            )
        )
    ]
    in_s = pltpu.make_async_copy(s_in, xs.at[z, xh, c], i_sem.at[0])
    in_t = pltpu.make_async_copy(t_in, ts.at[z, xh, c], i_sem.at[1])
    in_s.start()
    in_t.start()
    for load in loads:
        load.start()

    def put(i, src, dst):
        copy = pltpu.make_async_copy(src, dst, o_sem.at[i])
        copy.start()
        late.append(copy.wait)

    barrier = pltpu.get_barrier_semaphore()

    def greet(dev):
        pl.semaphore_signal(barrier, inc=1, device_id=dev, device_id_type=pl.DeviceIdType.MESH)

    greet(other)
    loop(1, G, lambda k: greet(grp_to(k)))
    loop(1, N, lambda k: greet(tp_to(k)))
    pl.semaphore_wait(barrier, 1 + G - 1 + N - 1)

    def at_block(zz, xx, cc):
        return (zz, xx, cc)

    in_s.wait()
    tp_ag_start(0, xs, at_block)
    in_t.wait()
    tp_ag_start(1, ts, at_block)

    def compact(blocks, tmp, rows):
        def one(i):
            for q in range(2 * XH):
                tmp[q * RB : (q + 1) * RB, :] = blocks[i, q // 2, q % 2].astype(FL)
            rows[pl.ds(pl.multiple_of(i * RZ, 16), RZ), :] = tmp[...].astype(BF)

        loop(0, Z, one)

    tp_ag_forward(0, xs, at_block)
    tp_ag_wait(0, xs, at_block)
    compact(xs, xtmp, x)
    put(0, x, o_x)

    for i in range(4):
        loads[i].wait()
    rows_g = x.shape[0] // G
    half = x.shape[0]
    n0 = 0
    while n0 < 2 * FS_L:
        n1 = min(n0 + 256, 2 * FS_L)
        out = dot(x[...], w_sp[n0:n1, :], 1, 1).astype(BF)
        for i in range(G):
            s2s[i, :, n0:n1] = out[i * rows_g : (i + 1) * rows_g]
        n0 = n1
    grp_rs_start(0, s2s, s2r)

    tp_ag_forward(1, ts, at_block)
    loads[6].wait()
    FT_L, BT = w_td.shape
    for j in range(BT // 128):
        w_tdt[j * 128 : (j + 1) * 128, :] = w_td[:, j * 128 : (j + 1) * 128].T
    tp_ag_wait(1, ts, at_block)
    compact(ts, ttmp, tx)
    loads[4].wait()
    loads[5].wait()
    for j, w in enumerate((w_tg, w_tu)):
        n0 = 0
        while n0 < FT_L:
            n1 = min(n0 + 256, FT_L)
            out = dot(tx[...], w[:, n0:n1], 1, 0).astype(BF)
            for i in range(G):
                t2s[i, j, :, n0:n1] = out[i * rows_g : (i + 1) * rows_g]
            n0 = n1

    acc = grp_rs_sum(0, s2s, s2r)
    pv[:, : 2 * A] = acc[:, : 2 * A]
    pv[:, 2 * A : 2 * FS_L] = acc[:, 2 * A :]
    pv[:, 2 * FS_L :] = pltpu.roll(acc[:, 2 * A :], B, 1)

    def pair_values():
        return ((pv[:, :A], pv[:, A : 2 * A], slice(0, A)),
                (pv[:, 2 * A : 2 * FS_L], pv[:, 2 * FS_L :], slice(A, FS_L)))

    for gate, up, cols in pair_values():
        value = (gate * jax.nn.sigmoid(gate) * up).astype(BF)
        h[g, :, cols] = value[:, : cols.stop - cols.start]

    def at_g(i):
        return (i,)

    grp_ag_start(1, h, at_g)
    grp_rs_start(2, t2s, t2r)
    grp_ag_wait(1, h, at_g)
    put(1, h, o_h)

    def all_sum_start(ph, part, keep, cs, cr):
        w = part.shape[1] // 2
        for j in range(2):
            keep[j] = part[:, j * w : (j + 1) * w]
            cs[j] = part[:, j * w : (j + 1) * w].astype(BF)
        c_start(ph, cs.at[o], cr)

    def all_sum_scatter(ph, tph, keep, cs, cr, rs, rr):
        c_copy(ph, cs.at[o], cr).wait_recv()
        q = cr.shape[1] // XH
        for i in range(Z):
            rows = slice(i * RZ, (i + 1) * RZ)
            both = keep[c, rows, :] + cr[rows, :].astype(FL)
            for j in range(XH):
                rs[i * XH + j] = both[:, j * q : (j + 1) * q].astype(BF)
        tp_rs_start(tph, rs, rr)

    Q = f.shape[1] // (2 * XH)

    def at_tile(zz, xx, cc):
        return (
            pl.ds(pl.multiple_of(zz * RZ, 16), RZ),
            pl.ds(pl.multiple_of((cc * XH + xx) * Q, Q), Q),
        )

    loads[7].wait()
    hh = h[...].reshape(half, h.shape[2])
    all_sum_start(0, dot(hh, w_sd[...], 1, 0), f_keep, f_cs, f_cr)
    all_sum_scatter(0, 2, f_keep, f_cs, f_cr, f_rs, f_rr)
    f[at_tile(z, xh, c)] = tp_rs_sum(2, f_rs, f_rr).astype(BF)
    tp_ag_start(3, f, at_tile)

    t2a[...] = t2s[g].astype(FL)

    def t2_add(k):
        grp_rs_copy(2, k, t2s, t2r).wait_recv()
        t2a[...] += t2r[k - 1].astype(FL)

    loop(1, G, t2_add)
    t_pre = t2a[0]
    th[g] = (t_pre * jax.nn.sigmoid(t_pre) * t2a[1]).astype(BF)
    grp_ag_start(3, th, at_g)

    tp_ag_forward(3, f, at_tile)
    tp_ag_wait(3, f, at_tile)
    put(2, f, o_f)

    loads[8].wait()
    p_part = dot(w_pt[...], f[...], 1, 1).astype(BF)
    O = p_s.shape[1]
    for i in range(G):
        p_s[i] = p_part[i * O : (i + 1) * O]
    grp_rs_start(4, p_s, p_r)

    grp_ag_wait(3, th, at_g)
    thh = th[...].reshape(half, th.shape[2])
    per = BT // Z
    for i in range(Z):
        part = dot(w_tdt[i * per : (i + 1) * per, :], thh, 1, 1)
        for j in range(XH):
            for m in range(2):
                block = part[(j * 2 + m) * O : (j * 2 + m + 1) * O]
                tf_keep[m, i * XH + j] = block
                tf_cs[m, i * XH + j] = block.astype(BF)
    c_start(1, tf_cs.at[o], tf_cr)
    c_copy(1, tf_cs.at[o], tf_cr).wait_recv()
    for i in range(N):
        tf_rs[i] = (tf_keep[c, i] + tf_cr[i].astype(FL)).astype(BF)
    tp_rs_start(4, tf_rs, tf_rr)
    projected = grp_rs_sum(4, p_s, p_r)
    tf[...] = tp_rs_sum(4, tf_rs, tf_rr)

    rt[g] = (projected - tf[...].astype(BF).astype(FL)).astype(BF)
    grp_ag_start(5, rt, at_g)
    grp_ag_wait(5, rt, at_g)
    put(3, rt, o_rt)

    rtt = rt[...].reshape(G * O, half)
    all_sum_start(2, dot(rtt.T, w_pt[...], 1, 0), g_keep, g_cs, g_cr)
    all_sum_scatter(2, 5, g_keep, g_cs, g_cr, g_rs, g_rr)
    fg[at_tile(z, xh, c)] = tp_rs_sum(5, g_rs, g_rr).astype(BF)
    tp_ag_start(6, fg, at_tile)
    tp_ag_forward(6, fg, at_tile)
    tp_ag_wait(6, fg, at_tile)
    put(4, fg, o_fg)

    h_part = dot(fg[...], w_sd[...], 1, 1).astype(BF)
    for i in range(G):
        h_s[i] = h_part[i * rows_g : (i + 1) * rows_g]
    grp_rs_start(6, h_s, h_r)
    hidden_grad = grp_rs_sum(6, h_s, h_r)
    (gate, up, _), (gate_2, up_2, _) = pair_values()

    def pair_grads(grad, gate, up):
        s = jax.nn.sigmoid(gate)
        return grad * up * s * (1.0 + gate * (1.0 - s)), grad * gate * s

    gate_grad, up_grad = pair_grads(hidden_grad[:, :A], gate, up)
    gu[g, :, :A] = gate_grad.astype(BF)
    gu[g, :, A : 2 * A] = up_grad.astype(BF)
    rest = jnp.concatenate([hidden_grad[:, A:], hidden_grad[:, A:]], axis=1)
    gate_grad, up_grad = pair_grads(rest, gate_2, up_2)
    lane = lax.broadcasted_iota(jnp.int32, gate_grad.shape, 1)
    gu[g, :, 2 * A :] = jnp.where(lane < B, gate_grad, pltpu.roll(up_grad, B, 1)).astype(BF)

    grp_ag_start(7, gu, at_g)
    grp_ag_wait(7, gu, at_g)
    gur = gu[...].reshape(half, 2 * FS_L)

    gi_part = dot(gur, w_sp[...], 1, 0)
    gi_f[...] = gi_part.reshape(gi_f.shape)
    last = gur[:, 2 * A :]
    gg[:, :A] = gur[:, :A]
    gg[:, A:] = last[:, :B]
    ug[:, :A] = gur[:, A : 2 * A]
    ug[:, A:] = last[:, B:]
    put(5, gg, o_gg)
    put(7, ug, o_ug)

    def spread(i):
        for j in range(XH):
            for m in range(2):
                q = j * 2 + m
                gi_cs[m, i * XH + j] = gi_f[i, q * RB : (q + 1) * RB, :].astype(BF)

    loop(0, Z, spread)
    c_start(3, gi_cs.at[o], gi_cr)
    c_copy(3, gi_cs.at[o], gi_cr).wait_recv()

    def pair_sum(i):
        gi_rs[i] = (gi_cs[c, i].astype(FL) + gi_cr[i].astype(FL)).astype(BF)

    loop(0, N, pair_sum)
    tp_rs_start(7, gi_rs, gi_rr)
    gi[...] = tp_rs_sum(7, gi_rs, gi_rr)
    put(6, gi, o_gi)
    for wait in late:
        wait()


def body(
    sizes,
    teacher_in,
    teacher_gate,
    teacher_up,
    teacher_down,
    student_in,
    student_gate,
    student_up,
    student_down,
    projector,
):
    Y, XL, Z, XH = sizes
    G, N = Y * XL, Z * XH
    rb, kt = teacher_in.shape
    ft = teacher_gate.shape[1]
    bt = teacher_down.shape[1]
    ks = student_in.shape[1]
    fs = student_gate.shape[1]
    ds = student_down.shape[1]
    off = projector.shape[2]
    R = rb * N * 2
    rz, rg = R // Z, R // G
    q = ds // (2 * XH)
    proj_t = projector.transpose(1, 2, 0).reshape(-1, projector.shape[0])
    A = fs // 128 * 128
    V = pltpu.VMEM
    D = pltpu.SemaphoreType.DMA
    pair = lambda dt: [
        V((2, R, ds // 2), FL), V((2, R, ds // 2), dt), V((R, ds // 2), dt),
        V((N, rz, q), dt), V((N - 1, rz, q), dt), V((R, ds), dt),
    ]
    scratch = [
        V((kt, ft), BF), V((kt, ft), BF), V((ft, bt), BF), V((bt, ft), BF),
        V((2 * fs, ks), BF), V((fs, ds), BF), V((G * off, ds), BF),
        V((Z, XH, 2, rb, ks), BF), V((rz, ks), FL), V((R, ks), BF),
        V((G, rg, 2 * fs), BF), V((G - 1, rg, 2 * fs), BF), V((rg, 4 * fs - 2 * A), FL),
        V((G, rg, fs), BF),
        *pair(BF),
        V((G, off, R), BF), V((G - 1, off, R), BF), V((G, off, R), BF),
        *pair(BF),
        V((G, rg, fs), BF), V((G - 1, rg, fs), BF), V((G, rg, 2 * fs), BF), V((R, fs), BF), V((R, fs), BF),
        V((Z, rz, ks), FL), V((2, N, rb, ks), BF), V((N, rb, ks), BF), V((N, rb, ks), BF),
        V((N - 1, rb, ks), BF), V((rb, ks), FL),
        V((Z, XH, 2, rb, kt), BF), V((rz, kt), FL), V((R, kt), BF),
        V((G, 2, rg, ft), BF), V((G - 1, 2, rg, ft), BF), V((2, rg, ft), FL), V((G, rg, ft), BF),
        V((2, N, off, R), FL), V((2, N, off, R), BF), V((N, off, R), BF), V((N, off, R), BF),
        V((N - 1, off, R), BF), V((off, R), FL),
        D((9,)), D((2,)), D((8,)), D((8, G)), D((8, G)), D((8, N)), D((8, N)),
        D((8, N)), D((8, N)), D((4,)), D((4,)),
    ]
    S = jax.ShapeDtypeStruct
    x, h, f, rt, fg, gg, ug, gi = pl.pallas_call(
        functools.partial(kernel, sizes),
        out_shape=(
            S((R, ks), BF), S((G, rg, fs), BF), S((R, ds), BF), S((G, off, R), BF),
            S((R, ds), BF), S((R, fs), BF), S((R, fs), BF), S((rb, ks), FL),
        ),
        in_specs=[pl.BlockSpec(memory_space=pl.ANY)] * 9,
        out_specs=tuple([pl.BlockSpec(memory_space=pl.ANY)] * 8),
        scratch_shapes=scratch,
        compiler_params=pltpu.CompilerParams(
            collective_id=0, has_side_effects=True, vmem_limit_bytes=60 * 1024 * 1024
        ),
        name="chain",
    )(
        teacher_in, teacher_gate, teacher_up, teacher_down,
        student_in, student_gate.T, student_up.T, student_down, proj_t,
    )
    h = h.reshape(R, fs)
    grad_projector = dot(rt.reshape(G * off, R), f, 1, 0).reshape(G, off, ds).transpose(2, 0, 1)
    grad_down = dot(h, fg, 0, 0)
    grad_gate = dot(gg, x, 0, 0).T
    grad_up = dot(ug, x, 0, 0).T
    return gi, grad_gate, grad_up, grad_down, grad_projector


def solution(mesh, sizes=(4, 2, 8, 2)):
    torus = Mesh(mesh.devices.reshape(*sizes, 2), AXES)
    in_specs = (
        P(TP, GRP),
        P(GRP, TP),
        P(GRP, TP),
        P(TP, GRP),
        P(TP, GRP),
        P(GRP, TP),
        P(GRP, TP),
        P(TP, GRP),
        P(GRP, None, TP),
    )
    out_specs = (P(TP, GRP), P(GRP, TP), P(GRP, TP), P(TP, GRP), P(GRP, None, TP))
    return jax.shard_map(
        functools.partial(body, sizes), mesh=torus, in_specs=in_specs, out_specs=out_specs, check_vma=False
    )
```

time: 371 us -> 162 us (0.44)
  the two profiles are of different devices: /device:TPU:53 before, /device:TPU:3 now
where the time goes in v1:
time: 162 us; the launch traced here: 161 us
  Pallas kernels  153 us (94%)
  matrix products  7.5 us (5%)
    pallas_call x1, Pallas kernels, body(): pl.pallas_call(functools.partial(kernel, sizes), out_shape=(S((R, ks), BF...  153 us
    dot_general x4, matrix products, dot(): lax.dot_general(a, b, (((ca,), (cb,)), ((), ())), preferred_element_type=FL)  7.5 us

profile of v1, /device:TPU:3, one launch (start us, length us, event | category | flops | bytes accessed | tf_op | source)
XLA Modules:
  0.0 161.4 jit_solution(8404427304755573394)
XLA Ops:
  0.6 152.7 %chain.1 = (bf16[384,512]{1,0:T(8,128)(2,1)}, bf16[8,48,448]{2,1,0:T(8,128)(2,1)}, bf16[384,512]{1,0:T(8,128)(2,1)}, bf16[8,32,384]{2,1,0:T(8,128)(2,1)}, bf16[3...) custom-call(bf16[12,1024]{1,0:T(8,128)(2,1)} %t_in.1, ...), custom_call_target="tpu_custom_call" | custom-call | tf_op jit(solution)/shard_map/chain/pallas_call | solution.py:468
  153.3 0.0 copy-start
  153.3 0.0 copy-start.3
  153.3 2.2 %fusion = f32[512,8,32]{0,2,1:T(8,128)} fusion(bf16[8,32,384]{2,1,0:T(8,128)(2,1)} %get-tuple-element.20, bf16[384,512]{1,0:T(8,128)(2,1)} %get-tuple-element.19), kind=kOutput, calls=%fused_computation | convolution fusion | flops 100663296 | bytes 1114112 | tf_op jit(solution)/shard_map/dot_general | solution.py:19
  155.5 0.0 copy-start.1
  155.5 0.0 copy-start.2
  155.5 2.6 %fusion.2 = f32[512,448]{0,1:T(8,128)} fusion(bf16[384,512]{1,0:T(8,128)(2,1)} %get-tuple-element.14, bf16[384,448]{1,0:T(8,128)(2,1)} %get-tuple-element.15), kind=kOutput, calls=%fused_computation.2 | convolution fusion | flops 176160768 | bytes 1654784 | tf_op jit(solution)/shard_map/dot_general | solution.py:19
  158.1 0.0 copy-done
  158.1 0.0 copy-done.3
  158.1 0.0 copy-start.4
  158.1 1.4 fusion.3
  159.5 0.0 copy-done.1
  159.5 0.0 copy-done.2
  159.5 1.3 fusion.4
  160.8 0.0 copy-done.4
  160.8 0.6 copy.15
Async XLA Ops:
  153.3 4.8 %copy-start = (bf16[384,512]{1,0:T(8,128)(2,1)S(1)}, bf16[384,512]{1,0:T(8,128)(2,1)}, u32[]{:S(2)}) copy-start(bf16[384,512]{1,0:T(8,128)(2,1)} %get-tuple-element.14) | copy-start | bytes 1179652
  153.3 4.8 %copy-start.3 = (bf16[384,448]{1,0:T(8,128)(2,1)S(1)}, bf16[384,448]{1,0:T(8,128)(2,1)}, u32[]{:S(2)}) copy-start(bf16[384,448]{1,0:T(8,128)(2,1)} %get-tuple-element.16) | copy-start | bytes 1032196
  155.5 4.0 %copy-start.1 = (bf16[8,48,448]{2,1,0:T(8,128)(2,1)S(1)}, bf16[8,48,448]{2,1,0:T(8,128)(2,1)}, u32[]{:S(2)}) copy-start(bf16[8,48,448]{2,1,0:T(8,128)(2,1)} %get-tuple-element.17) | copy-start | bytes 1032196
  155.5 4.0 %copy-start.2 = (bf16[384,512]{1,0:T(8,128)(2,1)S(1)}, bf16[384,512]{1,0:T(8,128)(2,1)}, u32[]{:S(2)}) copy-start(bf16[384,512]{1,0:T(8,128)(2,1)} %get-tuple-element.18) | copy-start | bytes 1179652
  158.1 2.7 %copy-start.4 = (f32[12,512]{1,0:T(8,128)S(1)}, f32[12,512]{1,0:T(8,128)}, u32[]{:S(2)}) copy-start(f32[12,512]{1,0:T(8,128)} %get-tuple-element.26) | copy-start | bytes 73732

commit v2 on v1

--- a/solution.py
+++ b/solution.py
@@ -22,13 +22,13 @@
 def kernel(
     sizes,
     t_in, t_gate, t_up, t_down, s_in, s_gate, s_up, s_down, proj_t,
-    o_x, o_h, o_f, o_rt, o_fg, o_gg, o_ug, o_gi,
+    o_gp, o_gd, o_gg, o_ug, o_gi,
     w_tg, w_tu, w_td, w_tdt, w_sp, w_sd, w_pt,
     xs, xtmp, x, s2s, s2r, pv, h,
     f_keep, f_cs, f_cr, f_rs, f_rr, f,
     p_s, p_r, rt,
     g_keep, g_cs, g_cr, g_rs, g_rr, fg,
-    h_s, h_r, gu, gg, ug,
+    h_s, h_r, gu, v_gp, v_gd, v_gg, v_ug,
     gi_f, gi_cs, gi_cr, gi_rs, gi_rr, gi,
     ts, ttmp, tx, t2s, t2r, t2a, th,
     tf_keep, tf_cs, tf_cr, tf_rs, tf_rr, tf,
@@ -165,6 +165,59 @@
     def grp_rs_sum(ph, send, recv):
         return summed(G, lambda k: grp_rs_copy(ph, k, send, recv), recv, send[g].astype(FL))
 
+    def lagged(order, first, second):
+        first(order[0])
+        for before, now in zip(order, order[1:]):
+            first(now)
+            second(before)
+        second(order[-1])
+
+    Z_ORDER = sorted(range(Z), key=lambda d: min(d, Z - d))
+    G_ORDER = sorted(range(G), key=lambda k: min(k // XL, Y - k // XL) + k % XL)
+
+    def tp_arrive(ph, buf, at, dz):
+        for k in range(dz * XH, (dz + 1) * XH):
+            if k:
+                zz, xx = tp_from(k)
+                block = buf.at[at(zz, xx, c)]
+                rdma(block, block, tp_ss.at[ph, k], tp_rs.at[ph, k], tp_to(k)).wait_recv()
+                rdma(block, block, fw_ss.at[ph, k], fw_rs.at[ph, k], other).start()
+
+    def tp_arrived(ph, buf, at, dz):
+        for k in range(dz * XH, (dz + 1) * XH):
+            zz, xx = tp_from(k)
+            block = buf.at[at(zz, xx, o)]
+            rdma(block, block, fw_ss.at[ph, k], fw_rs.at[ph, k], other).wait_recv()
+        return lax.rem(z + Z - dz, Z)
+
+    def grp_send(ph, i, send, recv):
+        k = lax.rem(i // XL + Y - y, Y) * XL + lax.rem(lax.rem(i, XL) + XL - xl, XL)
+
+        @pl.when(k != 0)
+        def _():
+            grp_rs_copy(ph, k, send, recv).start()
+
+    def grp_sent(ph, send, recv):
+        late.append(lambda: loop(1, G, lambda k: grp_rs_copy(ph, k, send, recv).wait_send()))
+
+    def tp_send(ph, i, j, send, recv):
+        k = lax.rem(i + Z - z, Z) * XH + lax.rem(j + XH - xh, XH)
+
+        @pl.when(k != 0)
+        def _():
+            tp_rs_copy(ph, k, send, recv).start()
+
+    def tp_sent(ph, send, recv):
+        late.append(lambda: loop(1, N, lambda k: tp_rs_copy(ph, k, send, recv).wait_send()))
+
+    def grp_arrived(ph, buf, k):
+        src = grp_from(k)
+        if k:
+            rdma(
+                buf.at[src], buf.at[src], grp_ss.at[ph, k], grp_rs.at[ph, k], grp_to(k)
+            ).wait_recv()
+        return src
+
     FS_L = s_gate.shape[0]
     A = FS_L // 128 * 128
     B = FS_L - A
@@ -208,49 +261,49 @@
     in_t.wait()
     tp_ag_start(1, ts, at_block)
 
-    def compact(blocks, tmp, rows):
-        def one(i):
-            for q in range(2 * XH):
-                tmp[q * RB : (q + 1) * RB, :] = blocks[i, q // 2, q % 2].astype(FL)
-            rows[pl.ds(pl.multiple_of(i * RZ, 16), RZ), :] = tmp[...].astype(BF)
-
-        loop(0, Z, one)
-
-    tp_ag_forward(0, xs, at_block)
-    tp_ag_wait(0, xs, at_block)
-    compact(xs, xtmp, x)
-    put(0, x, o_x)
-
-    for i in range(4):
-        loads[i].wait()
     rows_g = x.shape[0] // G
     half = x.shape[0]
-    n0 = 0
-    while n0 < 2 * FS_L:
-        n1 = min(n0 + 256, 2 * FS_L)
-        out = dot(x[...], w_sp[n0:n1, :], 1, 1).astype(BF)
-        for i in range(G):
-            s2s[i, :, n0:n1] = out[i * rows_g : (i + 1) * rows_g]
-        n0 = n1
-    grp_rs_start(0, s2s, s2r)
-
-    tp_ag_forward(1, ts, at_block)
+    O = p_s.shape[1]
+
+    def compact(blocks, tmp, i):
+        for q in range(2 * XH):
+            tmp[q * RB : (q + 1) * RB, :] = blocks[i, q // 2, q % 2].astype(FL)
+        return tmp[...].astype(BF)
+
     loads[6].wait()
     FT_L, BT = w_td.shape
     for j in range(BT // 128):
         w_tdt[j * 128 : (j + 1) * 128, :] = w_td[:, j * 128 : (j + 1) * 128].T
-    tp_ag_wait(1, ts, at_block)
-    compact(ts, ttmp, tx)
-    loads[4].wait()
-    loads[5].wait()
-    for j, w in enumerate((w_tg, w_tu)):
-        n0 = 0
-        while n0 < FT_L:
-            n1 = min(n0 + 256, FT_L)
-            out = dot(tx[...], w[:, n0:n1], 1, 0).astype(BF)
-            for i in range(G):
-                t2s[i, j, :, n0:n1] = out[i * rows_g : (i + 1) * rows_g]
-            n0 = n1
+    for i in range(6):
+        loads[i].wait()
+
+    def s_use(dz):
+        i = tp_arrived(0, xs, at_block, dz)
+        rows = compact(xs, xtmp, i)
+        x[pl.ds(pl.multiple_of(i * RZ, 16), RZ), :] = rows
+        s2s[i] = dot(rows, w_sp[...], 1, 1).astype(BF)
+        grp_send(0, i, s2s, s2r)
+
+    lagged(Z_ORDER, lambda dz: tp_arrive(0, xs, at_block, dz), s_use)
+    grp_sent(0, s2s, s2r)
+
+    def t_use(pair):
+        blocks = [tp_arrived(1, ts, at_block, dz) for dz in pair]
+        rows = jnp.concatenate([compact(ts, ttmp, i) for i in blocks], axis=0)
+        for j, w in enumerate((w_tg, w_tu)):
+            out = dot(rows, w[...], 1, 0).astype(BF)
+            for n, i in enumerate(blocks):
+                t2s[i, j] = out[n * RZ : (n + 1) * RZ]
+        for i in blocks:
+            grp_send(2, i, t2s, t2r)
+
+    def t_arrive(pair):
+        for dz in pair:
+            tp_arrive(1, ts, at_block, dz)
+
+    pairs = [Z_ORDER[i : i + 2] for i in range(0, Z, 2)]
+    cut = (len(pairs) + 1) // 2
+    lagged(pairs[:cut], t_arrive, t_use)
 
     acc = grp_rs_sum(0, s2s, s2r)
     pv[:, : 2 * A] = acc[:, : 2 * A]
@@ -269,28 +322,12 @@
         return (i,)
 
     grp_ag_start(1, h, at_g)
-    grp_rs_start(2, t2s, t2r)
-    grp_ag_wait(1, h, at_g)
-    put(1, h, o_h)
-
-    def all_sum_start(ph, part, keep, cs, cr):
-        w = part.shape[1] // 2
-        for j in range(2):
-            keep[j] = part[:, j * w : (j + 1) * w]
-            cs[j] = part[:, j * w : (j + 1) * w].astype(BF)
-        c_start(ph, cs.at[o], cr)
-
-    def all_sum_scatter(ph, tph, keep, cs, cr, rs, rr):
-        c_copy(ph, cs.at[o], cr).wait_recv()
-        q = cr.shape[1] // XH
-        for i in range(Z):
-            rows = slice(i * RZ, (i + 1) * RZ)
-            both = keep[c, rows, :] + cr[rows, :].astype(FL)
-            for j in range(XH):
-                rs[i * XH + j] = both[:, j * q : (j + 1) * q].astype(BF)
-        tp_rs_start(tph, rs, rr)
+    if pairs[cut:]:
+        lagged(pairs[cut:], t_arrive, t_use)
+    grp_sent(2, t2s, t2r)
 
     Q = f.shape[1] // (2 * XH)
+    W = f.shape[1] // 2
 
     def at_tile(zz, xx, cc):
         return (
@@ -298,12 +335,33 @@
             pl.ds(pl.multiple_of((cc * XH + xx) * Q, Q), Q),
         )
 
+    def pair_send(cph, part, i, keep, cs, cr):
+        for m in range(2):
+            keep[m, i] = part[:, m * W : (m + 1) * W]
+            cs[m, i] = part[:, m * W : (m + 1) * W].astype(BF)
+        c_copy((cph, i), cs.at[o, i], cr.at[i]).start()
+
+    def pair_sent(cph, cs, cr):
+        late.append(lambda: loop(0, Z, lambda i: c_copy((cph, i), cs.at[o, i], cr.at[i]).wait_send()))
+
+    def scatter_send(cph, tph, i, keep, cs, cr, rs, rr):
+        c_copy((cph, i), cs.at[o, i], cr.at[i]).wait_recv()
+        both = keep[c, i] + cr[i].astype(FL)
+        for j in range(XH):
+            rs[i * XH + j] = both[:, j * Q : (j + 1) * Q].astype(BF)
+            tp_send(tph, i, j, rs, rr)
+
     loads[7].wait()
-    hh = h[...].reshape(half, h.shape[2])
-    all_sum_start(0, dot(hh, w_sd[...], 1, 0), f_keep, f_cs, f_cr)
-    all_sum_scatter(0, 2, f_keep, f_cs, f_cr, f_rs, f_rr)
-    f[at_tile(z, xh, c)] = tp_rs_sum(2, f_rs, f_rr).astype(BF)
-    tp_ag_start(3, f, at_tile)
+
+    def s4_first(k):
+        i = grp_arrived(1, h, k)
+        pair_send(0, dot(h[i], w_sd[...], 1, 0), i, f_keep, f_cs, f_cr)
+
+    lagged(
+        G_ORDER, s4_first, lambda k: scatter_send(0, 2, grp_from(k), f_keep, f_cs, f_cr, f_rs, f_rr)
+    )
+    pair_sent(0, f_cs, f_cr)
+    tp_sent(2, f_rs, f_rr)
 
     t2a[...] = t2s[g].astype(FL)
 
@@ -316,16 +374,8 @@
     th[g] = (t_pre * jax.nn.sigmoid(t_pre) * t2a[1]).astype(BF)
     grp_ag_start(3, th, at_g)
 
-    tp_ag_forward(3, f, at_tile)
-    tp_ag_wait(3, f, at_tile)
-    put(2, f, o_f)
-
-    loads[8].wait()
-    p_part = dot(w_pt[...], f[...], 1, 1).astype(BF)
-    O = p_s.shape[1]
-    for i in range(G):
-        p_s[i] = p_part[i * O : (i + 1) * O]
-    grp_rs_start(4, p_s, p_r)
+    f[at_tile(z, xh, c)] = tp_rs_sum(2, f_rs, f_rr).astype(BF)
+    tp_ag_start(3, f, at_tile)
 
     grp_ag_wait(3, th, at_g)
     thh = th[...].reshape(half, th.shape[2])
@@ -337,32 +387,51 @@
                 block = part[(j * 2 + m) * O : (j * 2 + m + 1) * O]
                 tf_keep[m, i * XH + j] = block
                 tf_cs[m, i * XH + j] = block.astype(BF)
-    c_start(1, tf_cs.at[o], tf_cr)
-    c_copy(1, tf_cs.at[o], tf_cr).wait_recv()
+    c_start((1, 0), tf_cs.at[o], tf_cr)
+
+    tp_ag_forward(3, f, at_tile)
+    c_copy((1, 0), tf_cs.at[o], tf_cr).wait_recv()
     for i in range(N):
         tf_rs[i] = (tf_keep[c, i] + tf_cr[i].astype(FL)).astype(BF)
     tp_rs_start(4, tf_rs, tf_rr)
+
+    tp_ag_wait(3, f, at_tile)
+
+    loads[8].wait()
+    p_part = dot(w_pt[...], f[...], 1, 1).astype(BF)
+    for i in range(G):
+        p_s[i] = p_part[i * O : (i + 1) * O]
+    grp_rs_start(4, p_s, p_r)
+
     projected = grp_rs_sum(4, p_s, p_r)
     tf[...] = tp_rs_sum(4, tf_rs, tf_rr)
 
     rt[g] = (projected - tf[...].astype(BF).astype(FL)).astype(BF)
     grp_ag_start(5, rt, at_g)
     grp_ag_wait(5, rt, at_g)
-    put(3, rt, o_rt)
 
     rtt = rt[...].reshape(G * O, half)
-    all_sum_start(2, dot(rtt.T, w_pt[...], 1, 0), g_keep, g_cs, g_cr)
-    all_sum_scatter(2, 5, g_keep, g_cs, g_cr, g_rs, g_rr)
+    rtn = rtt.T
+    for i in range(Z):
+        pair_send(2, dot(rtn[i * RZ : (i + 1) * RZ], w_pt[...], 1, 0), i, g_keep, g_cs, g_cr)
+    for i in range(Z):
+        scatter_send(2, 5, i, g_keep, g_cs, g_cr, g_rs, g_rr)
+    pair_sent(2, g_cs, g_cr)
+    tp_sent(5, g_rs, g_rr)
+    v_gp[...] = dot(rtt, f[...], 1, 0)
+    put(0, v_gp, o_gp)
     fg[at_tile(z, xh, c)] = tp_rs_sum(5, g_rs, g_rr).astype(BF)
     tp_ag_start(6, fg, at_tile)
-    tp_ag_forward(6, fg, at_tile)
-    tp_ag_wait(6, fg, at_tile)
-    put(4, fg, o_fg)
-
-    h_part = dot(fg[...], w_sd[...], 1, 1).astype(BF)
-    for i in range(G):
-        h_s[i] = h_part[i * rows_g : (i + 1) * rows_g]
-    grp_rs_start(6, h_s, h_r)
+
+    def s8_use(dz):
+        i = tp_arrived(6, fg, at_tile, dz)
+        h_s[i] = dot(fg[pl.ds(pl.multiple_of(i * RZ, 16), RZ), :], w_sd[...], 1, 1).astype(BF)
+        grp_send(6, i, h_s, h_r)
+
+    lagged(Z_ORDER, lambda dz: tp_arrive(6, fg, at_tile, dz), s8_use)
+    grp_sent(6, h_s, h_r)
+    v_gd[...] = dot(h[...].reshape(half, FS_L).T, fg[...], 1, 0)
+    put(1, v_gd, o_gd)
     hidden_grad = grp_rs_sum(6, h_s, h_r)
     (gate, up, _), (gate_2, up_2, _) = pair_values()
 
@@ -379,38 +448,54 @@
     gu[g, :, 2 * A :] = jnp.where(lane < B, gate_grad, pltpu.roll(up_grad, B, 1)).astype(BF)
 
     grp_ag_start(7, gu, at_g)
-    grp_ag_wait(7, gu, at_g)
-    gur = gu[...].reshape(half, 2 * FS_L)
-
-    gi_part = dot(gur, w_sp[...], 1, 0)
-    gi_f[...] = gi_part.reshape(gi_f.shape)
-    last = gur[:, 2 * A :]
-    gg[:, :A] = gur[:, :A]
-    gg[:, A:] = last[:, :B]
-    ug[:, :A] = gur[:, A : 2 * A]
-    ug[:, A:] = last[:, B:]
-    put(5, gg, o_gg)
-    put(7, ug, o_ug)
-
-    def spread(i):
+
+    def s10_first(k):
+        i = grp_arrived(7, gu, k)
+        gi_f[...] = dot(gu[i], w_sp[...], 1, 0)
+        for m in range(2):
+            for j in range(XH):
+                q = j * 2 + m
+                gi_cs[m, i, j] = gi_f[q * RB : (q + 1) * RB, :].astype(BF)
+        c_copy((3, i), gi_cs.at[o, i], gi_cr.at[i]).start()
+
+    def s10_second(k):
+        i = grp_from(k)
+        c_copy((3, i), gi_cs.at[o, i], gi_cr.at[i]).wait_recv()
         for j in range(XH):
-            for m in range(2):
-                q = j * 2 + m
-                gi_cs[m, i * XH + j] = gi_f[i, q * RB : (q + 1) * RB, :].astype(BF)
-
-    loop(0, Z, spread)
-    c_start(3, gi_cs.at[o], gi_cr)
-    c_copy(3, gi_cs.at[o], gi_cr).wait_recv()
-
-    def pair_sum(i):
-        gi_rs[i] = (gi_cs[c, i].astype(FL) + gi_cr[i].astype(FL)).astype(BF)
-
-    loop(0, N, pair_sum)
-    tp_rs_start(7, gi_rs, gi_rr)
-    gi[...] = tp_rs_sum(7, gi_rs, gi_rr)
-    put(6, gi, o_gi)
+            gi_rs[i * XH + j] = (gi_cs[c, i, j].astype(FL) + gi_cr[i, j].astype(FL)).astype(BF)
+            tp_send(7, i, j, gi_rs, gi_rr)
+
+    lagged(G_ORDER, s10_first, s10_second)
+    pair_sent(3, gi_cs, gi_cr)
+    tp_sent(7, gi_rs, gi_rr)
+    gut = gu[...].reshape(half, 2 * FS_L).T
+    v_gg[:A] = dot(gut[:A], x[...], 1, 0)
+    v_gg[A:] = dot(gut[2 * A : 2 * A + B], x[...], 1, 0)
+    put(2, v_gg, o_gg)
+    v_ug[:A] = dot(gut[A : 2 * A], x[...], 1, 0)
+    v_ug[A:] = dot(gut[2 * A + B :], x[...], 1, 0)
+    put(3, v_ug, o_ug)
     for wait in late:
         wait()
+    late.clear()
+    gi[...] = tp_rs_sum(7, gi_rs, gi_rr)
+    put(4, gi, o_gi)
+    for wait in late:
+        wait()
+
+
+def finish(*refs):
+    n = len(refs) // 3
+    sources, results, held, sem = refs[:n], refs[n : 2 * n], refs[2 * n : 3 * n], refs[-1]
+    loads = [pltpu.make_async_copy(sources[i], held[i], sem.at[0, i]) for i in range(n)]
+    stores = [pltpu.make_async_copy(held[i], results[i], sem.at[1, i]) for i in range(n)]
+    for load in loads:
+        load.start()
+    for load, store in zip(loads, stores):
+        load.wait()
+        store.start()
+    for store in stores:
+        store.wait()
 
 
 def body(
@@ -442,7 +527,7 @@
     V = pltpu.VMEM
     D = pltpu.SemaphoreType.DMA
     pair = lambda dt: [
-        V((2, R, ds // 2), FL), V((2, R, ds // 2), dt), V((R, ds // 2), dt),
+        V((2, Z, rz, ds // 2), FL), V((2, Z, rz, ds // 2), dt), V((Z, rz, ds // 2), dt),
         V((N, rz, q), dt), V((N - 1, rz, q), dt), V((R, ds), dt),
     ]
     scratch = [
@@ -454,25 +539,24 @@
         *pair(BF),
         V((G, off, R), BF), V((G - 1, off, R), BF), V((G, off, R), BF),
         *pair(BF),
-        V((G, rg, fs), BF), V((G - 1, rg, fs), BF), V((G, rg, 2 * fs), BF), V((R, fs), BF), V((R, fs), BF),
-        V((Z, rz, ks), FL), V((2, N, rb, ks), BF), V((N, rb, ks), BF), V((N, rb, ks), BF),
+        V((G, rg, fs), BF), V((G - 1, rg, fs), BF), V((G, rg, 2 * fs), BF), V((G * off, ds), FL), V((fs, ds), FL), V((fs, ks), FL), V((fs, ks), FL),
+        V((rz, ks), FL), V((2, Z, XH, rb, ks), BF), V((Z, XH, rb, ks), BF), V((N, rb, ks), BF),
         V((N - 1, rb, ks), BF), V((rb, ks), FL),
         V((Z, XH, 2, rb, kt), BF), V((rz, kt), FL), V((R, kt), BF),
         V((G, 2, rg, ft), BF), V((G - 1, 2, rg, ft), BF), V((2, rg, ft), FL), V((G, rg, ft), BF),
         V((2, N, off, R), FL), V((2, N, off, R), BF), V((N, off, R), BF), V((N, off, R), BF),
         V((N - 1, off, R), BF), V((off, R), FL),
         D((9,)), D((2,)), D((8,)), D((8, G)), D((8, G)), D((8, N)), D((8, N)),
-        D((8, N)), D((8, N)), D((4,)), D((4,)),
+        D((8, N)), D((8, N)), D((4, Z)), D((4, Z)),
     ]
     S = jax.ShapeDtypeStruct
-    x, h, f, rt, fg, gg, ug, gi = pl.pallas_call(
+    grads = pl.pallas_call(
         functools.partial(kernel, sizes),
         out_shape=(
-            S((R, ks), BF), S((G, rg, fs), BF), S((R, ds), BF), S((G, off, R), BF),
-            S((R, ds), BF), S((R, fs), BF), S((R, fs), BF), S((rb, ks), FL),
+            S((G * off, ds), FL), S((fs, ds), FL), S((fs, ks), FL), S((fs, ks), FL), S((rb, ks), FL),
         ),
         in_specs=[pl.BlockSpec(memory_space=pl.ANY)] * 9,
-        out_specs=tuple([pl.BlockSpec(memory_space=pl.ANY)] * 8),
+        out_specs=tuple([pl.BlockSpec(memory_space=pl.ANY)] * 5),
         scratch_shapes=scratch,
         compiler_params=pltpu.CompilerParams(
             collective_id=0, has_side_effects=True, vmem_limit_bytes=60 * 1024 * 1024
@@ -482,12 +566,18 @@
         teacher_in, teacher_gate, teacher_up, teacher_down,
         student_in, student_gate.T, student_up.T, student_down, proj_t,
     )
-    h = h.reshape(R, fs)
-    grad_projector = dot(rt.reshape(G * off, R), f, 1, 0).reshape(G, off, ds).transpose(2, 0, 1)
-    grad_down = dot(h, fg, 0, 0)
-    grad_gate = dot(gg, x, 0, 0).T
-    grad_up = dot(ug, x, 0, 0).T
-    return gi, grad_gate, grad_up, grad_down, grad_projector
+    shapes = [(g.shape, g.dtype) for g in grads]
+    grad_projector, grad_down, grad_gate, grad_up, grad_input = pl.pallas_call(
+        finish,
+        out_shape=tuple(S(*shape) for shape in shapes),
+        in_specs=[pl.BlockSpec(memory_space=pl.ANY)] * 5,
+        out_specs=tuple([pl.BlockSpec(memory_space=pl.ANY)] * 5),
+        scratch_shapes=[*(V(*shape) for shape in shapes), D((2, 5))],
+        compiler_params=pltpu.CompilerParams(vmem_limit_bytes=60 * 1024 * 1024),
+        name="finish",
+    )(*grads)
+    grad_projector = grad_projector.reshape(G, off, ds).transpose(2, 0, 1)
+    return grad_input, grad_gate.T, grad_up.T, grad_down, grad_projector
 
 
 def solution(mesh, sizes=(4, 2, 8, 2)):

time: 162 us -> 151 us (0.932)
  the two profiles are of different devices: /device:TPU:3 before, /device:TPU:53 now
where the time goes in v2:
time: 151 us
  Pallas kernels  150 us (99%)
    pallas_call x1, Pallas kernels, body(): pl.pallas_call(functools.partial(kernel, sizes), out_shape=(S((G * off, d...  147 us

profile of v2, /device:TPU:53, one launch (start us, length us, event | category | flops | bytes accessed | tf_op | source)
XLA Modules:
  0.0 151.0 jit_solution(1909703957245245732)
XLA Ops:
  0.6 147.4 %chain.1 = (f32[256,512]{1,0:T(8,128)}, f32[448,512]{1,0:T(8,128)}, f32[448,512]{1,0:T(8,128)}, f32[448,512]{1,0:T(8,128)}, f32[12,512]{1,0:T(8,128)}) custom-call(bf16[12,1024]{1,0:T(8,128)(2,1)} %t_in.1, bf16[1024,896]{1,0:T(8,128)(2,1)} %t_gate.1, bf16[1024,896]{1,0:T(8,128)(2,1)} %t_up.1, bf16[896,1024]{1,0:T(8,128)(2,1)} %t_down.1, ...), custom_call_target="tpu_custom_call" | custom-call | tf_op jit(solution)/shard_map/chain/pallas_call | solution.py:553
  148.0 3.0 %finish.1 = (f32[256,512]{1,0:T(8,128)}, f32[448,512]{1,0:T(8,128)}, f32[448,512]{1,0:T(8,128)}, f32[448,512]{1,0:T(8,128)}, f32[12,512]{1,0:T(8,128)}) custom-call(f32[256,512]{1,0:T(8,128)} %get-tuple-element.15.refs_0_, f32[448,512]{1,0:T(8,128)} %get-tuple-element.16.refs_1_, f32[448,512]{1,0:T(8,128)} %get-tuple-element.17.refs_2_, ...), custom_call_target="tpu_custom_call" | custom-call | tf_op jit(solution)/shard_map/finish/pallas_call | solution.py:570

commit v3 on v2

--- a/solution.py
+++ b/solution.py
@@ -28,7 +28,7 @@
     f_keep, f_cs, f_cr, f_rs, f_rr, f,
     p_s, p_r, rt,
     g_keep, g_cs, g_cr, g_rs, g_rr, fg,
-    h_s, h_r, gu, v_gp, v_gd, v_gg, v_ug,
+    h_s, h_r, gu, v_rt, v_gp, v_gd, v_gg, v_ug,
     gi_f, gi_cs, gi_cr, gi_rs, gi_rr, gi,
     ts, ttmp, tx, t2s, t2r, t2a, th,
     tf_keep, tf_cs, tf_cr, tf_rs, tf_rr, tf,
@@ -76,6 +76,14 @@
 
     late = []
 
+    Z_FAR = sorted(range(Z), key=lambda d: -min(d, Z - d))
+    N_FAR = [d * XH + j for d in Z_FAR for j in reversed(range(XH)) if d + j]
+    G_FAR = sorted(range(1, G), key=lambda k: -min(k // XL, Y - k // XL) - k % XL)
+
+    def each(order, start):
+        for k in order:
+            start(k)
+
     def grp_rs_copy(ph, k, send, recv):
         to = grp_to(k)
         return rdma(
@@ -84,14 +92,14 @@
         )
 
     def grp_rs_start(ph, send, recv):
-        loop(1, G, lambda k: grp_rs_copy(ph, k, send, recv).start())
+        each(G_FAR, lambda k: grp_rs_copy(ph, k, send, recv).start())
         late.append(lambda: loop(1, G, lambda k: grp_rs_copy(ph, k, send, recv).wait_send()))
 
     def grp_ag_copy(ph, k, buf, at):
         return rdma(buf.at[at(g)], buf.at[at(g)], grp_ss.at[ph, k], grp_rs.at[ph, k], grp_to(k))
 
-    def grp_ag_start(ph, buf, at):
-        loop(1, G, lambda k: grp_ag_copy(ph, k, buf, at).start())
+    def grp_ag_start(ph, buf, at, order):
+        each(order, lambda k: grp_ag_copy(ph, k, buf, at).start())
         late.append(lambda: loop(1, G, lambda k: grp_ag_copy(ph, k, buf, at).wait_send()))
 
     def grp_ag_wait(ph, buf, at):
@@ -149,7 +157,7 @@
         )
 
     def tp_rs_start(ph, send, recv):
-        loop(1, N, lambda k: tp_rs_copy(ph, k, send, recv).start())
+        each(N_FAR, lambda k: tp_rs_copy(ph, k, send, recv).start())
         late.append(lambda: loop(1, N, lambda k: tp_rs_copy(ph, k, send, recv).wait_send()))
 
     def summed(n, copy, recv, first):
@@ -165,12 +173,12 @@
     def grp_rs_sum(ph, send, recv):
         return summed(G, lambda k: grp_rs_copy(ph, k, send, recv), recv, send[g].astype(FL))
 
-    def lagged(order, first, second):
-        first(order[0])
-        for before, now in zip(order, order[1:]):
-            first(now)
-            second(before)
-        second(order[-1])
+    def lagged(order, first, second, lag=1):
+        for n in range(len(order) + lag):
+            if n < len(order):
+                first(order[n])
+            if n >= lag:
+                second(order[n - lag])
 
     Z_ORDER = sorted(range(Z), key=lambda d: min(d, Z - d))
     G_ORDER = sorted(range(G), key=lambda k: min(k // XL, Y - k // XL) + k % XL)
@@ -321,7 +329,7 @@
     def at_g(i):
         return (i,)
 
-    grp_ag_start(1, h, at_g)
+    grp_ag_start(1, h, at_g, range(1, G))
     if pairs[cut:]:
         lagged(pairs[cut:], t_arrive, t_use)
     grp_sent(2, t2s, t2r)
@@ -372,50 +380,86 @@
     loop(1, G, t2_add)
     t_pre = t2a[0]
     th[g] = (t_pre * jax.nn.sigmoid(t_pre) * t2a[1]).astype(BF)
-    grp_ag_start(3, th, at_g)
+    grp_ag_start(3, th, at_g, G_FAR)
 
     f[at_tile(z, xh, c)] = tp_rs_sum(2, f_rs, f_rr).astype(BF)
     tp_ag_start(3, f, at_tile)
 
+    def s5_start():
+        tp_ag_wait(3, f, at_tile)
+        p_part = dot(w_pt[...], f[...], 1, 1).astype(BF)
+        for i in range(G):
+            p_s[i] = p_part[i * O : (i + 1) * O]
+        grp_rs_start(4, p_s, p_r)
+
+    loads[8].wait()
     grp_ag_wait(3, th, at_g)
     thh = th[...].reshape(half, th.shape[2])
     per = BT // Z
-    for i in range(Z):
-        part = dot(w_tdt[i * per : (i + 1) * per, :], thh, 1, 1)
-        for j in range(XH):
-            for m in range(2):
-                block = part[(j * 2 + m) * O : (j * 2 + m + 1) * O]
-                tf_keep[m, i * XH + j] = block
-                tf_cs[m, i * XH + j] = block.astype(BF)
-    c_start((1, 0), tf_cs.at[o], tf_cr)
-
+
+    def t4_pair(i):
+        return c_copy((1, i), tf_cs.at[o, i], tf_cr.at[i])
+
+    def t4_first(ds):
+        blocks = [lax.rem(z + d, Z) for d in ds]
+        rows = [w_tdt[pl.ds(pl.multiple_of(i * per, per), per), :] for i in blocks]
+        part = dot(jnp.concatenate(rows, axis=0), thh, 1, 1)
+        for n, i in enumerate(blocks):
+            for j in range(XH):
+                for m in range(2):
+                    at = n * per + (j * 2 + m) * O
+                    block = part[at : at + O]
+                    tf_keep[m, i, j] = block
+                    tf_cs[m, i, j] = block.astype(BF)
+            t4_pair(i).start()
+
+    def t4_second(ds):
+        for d in ds:
+            i = lax.rem(z + d, Z)
+            t4_pair(i).wait_recv()
+            for j in range(XH):
+                tf_rs[i * XH + j] = (tf_keep[c, i, j] + tf_cr[i, j].astype(FL)).astype(BF)
+                tp_send(4, i, j, tf_rs, tf_rr)
+
+    far = [Z_FAR[i : i + 2] for i in range(0, Z, 2)]
+    mid = max(1, len(far) // 2)
+    for n, ds in enumerate(far[:mid]):
+        t4_first(ds)
+        if n:
+            t4_second(far[n - 1])
     tp_ag_forward(3, f, at_tile)
-    c_copy((1, 0), tf_cs.at[o], tf_cr).wait_recv()
-    for i in range(N):
-        tf_rs[i] = (tf_keep[c, i] + tf_cr[i].astype(FL)).astype(BF)
-    tp_rs_start(4, tf_rs, tf_rr)
-
-    tp_ag_wait(3, f, at_tile)
-
-    loads[8].wait()
-    p_part = dot(w_pt[...], f[...], 1, 1).astype(BF)
-    for i in range(G):
-        p_s[i] = p_part[i * O : (i + 1) * O]
-    grp_rs_start(4, p_s, p_r)
+    for n in range(mid, len(far)):
+        t4_second(far[n - 1])
+        if n == len(far) - 1:
+            s5_start()
+        t4_first(far[n])
+    if mid == len(far):
+        s5_start()
+    t4_second(far[-1])
+    pair_sent(1, tf_cs, tf_cr)
+    tp_sent(4, tf_rs, tf_rr)
 
     projected = grp_rs_sum(4, p_s, p_r)
     tf[...] = tp_rs_sum(4, tf_rs, tf_rr)
 
     rt[g] = (projected - tf[...].astype(BF).astype(FL)).astype(BF)
-    grp_ag_start(5, rt, at_g)
+    grp_ag_start(5, rt, at_g, G_FAR)
     grp_ag_wait(5, rt, at_g)
 
     rtt = rt[...].reshape(G * O, half)
-    rtn = rtt.T
-    for i in range(Z):
-        pair_send(2, dot(rtn[i * RZ : (i + 1) * RZ], w_pt[...], 1, 0), i, g_keep, g_cs, g_cr)
-    for i in range(Z):
-        scatter_send(2, 5, i, g_keep, g_cs, g_cr, g_rs, g_rr)
+    v_rt[...] = rtt.T
+
+    def s7_first(d):
+        i = lax.rem(z + d, Z)
+        rows = v_rt[pl.ds(pl.multiple_of(i * RZ, 16), RZ), :]
+        pair_send(2, dot(rows, w_pt[...], 1, 0), i, g_keep, g_cs, g_cr)
+
+    lagged(
+        Z_FAR,
+        s7_first,
+        lambda d: scatter_send(2, 5, lax.rem(z + d, Z), g_keep, g_cs, g_cr, g_rs, g_rr),
+        lag=min(3, Z),
+    )
     pair_sent(2, g_cs, g_cr)
     tp_sent(5, g_rs, g_rr)
     v_gp[...] = dot(rtt, f[...], 1, 0)
@@ -447,7 +491,7 @@
     lane = lax.broadcasted_iota(jnp.int32, gate_grad.shape, 1)
     gu[g, :, 2 * A :] = jnp.where(lane < B, gate_grad, pltpu.roll(up_grad, B, 1)).astype(BF)
 
-    grp_ag_start(7, gu, at_g)
+    grp_ag_start(7, gu, at_g, range(1, G))
 
     def s10_first(k):
         i = grp_arrived(7, gu, k)
@@ -539,12 +583,12 @@
         *pair(BF),
         V((G, off, R), BF), V((G - 1, off, R), BF), V((G, off, R), BF),
         *pair(BF),
-        V((G, rg, fs), BF), V((G - 1, rg, fs), BF), V((G, rg, 2 * fs), BF), V((G * off, ds), FL), V((fs, ds), FL), V((fs, ks), FL), V((fs, ks), FL),
+        V((G, rg, fs), BF), V((G - 1, rg, fs), BF), V((G, rg, 2 * fs), BF), V((R, G * off), BF), V((G * off, ds), FL), V((fs, ds), FL), V((fs, ks), FL), V((fs, ks), FL),
         V((rz, ks), FL), V((2, Z, XH, rb, ks), BF), V((Z, XH, rb, ks), BF), V((N, rb, ks), BF),
         V((N - 1, rb, ks), BF), V((rb, ks), FL),
         V((Z, XH, 2, rb, kt), BF), V((rz, kt), FL), V((R, kt), BF),
         V((G, 2, rg, ft), BF), V((G - 1, 2, rg, ft), BF), V((2, rg, ft), FL), V((G, rg, ft), BF),
-        V((2, N, off, R), FL), V((2, N, off, R), BF), V((N, off, R), BF), V((N, off, R), BF),
+        V((2, Z, XH, off, R), FL), V((2, Z, XH, off, R), BF), V((Z, XH, off, R), BF), V((N, off, R), BF),
         V((N - 1, off, R), BF), V((off, R), FL),
         D((9,)), D((2,)), D((8,)), D((8, G)), D((8, G)), D((8, N)), D((8, N)),
         D((8, N)), D((8, N)), D((4, Z)), D((4, Z)),

time: 151 us -> 146 us (0.967); the launches traced: 151 us -> 144 us
  Pallas kernels: 150 us -> 143 us
    pallas_call x1, Pallas kernels: 147 us -> 140 us  [body(): pl.pallas_call(functools.partial(kernel, sizes), out_shape=(S((G * off, d...]
where the time goes in v3:
time: 146 us; the launch traced here: 144 us
  Pallas kernels  143 us (98%)
    pallas_call x1, Pallas kernels, body(): pl.pallas_call(functools.partial(kernel, sizes), out_shape=(S((G * off, d...  140 us
    pallas_call x1, Pallas kernels, body(): pl.pallas_call(finish, out_shape=tuple((S(*shape) for shape in shapes)),...  2.96 us

profile of v3, /device:TPU:53, one launch (start us, length us, event | category | flops | bytes accessed | tf_op | source)
XLA Modules:
  0.0 143.9 jit_solution(4172557895675997075)
XLA Ops:
  0.6 140.3 %chain.1 = (f32[256,512]{1,0:T(8,128)}, f32[448,512]{1,0:T(8,128)}, f32[448,512]{1,0:T(8,128)}, f32[448,512]{1,0:T(8,128)}, f32[12,512]{1,0:T(8,128)}) custom-call(bf16[12,1024]{1,0:T(8,128)(2,1)} %t_in.1, bf16[1024,896]{1,0:T(8,128)(2,1)} %t_gate.1, bf16[1024,896]{1,0:T(8,128)(2,1)} %t_up.1, bf16[896,1024]{1,0:T(8,128)(2,1)} %t_down.1, ...), custom_call_target="tpu_custom_call" | custom-call | tf_op jit(solution)/shard_map/chain/pallas_call | solution.py:597
  141.0 3.0 %finish.1 = (f32[256,512]{1,0:T(8,128)}, f32[448,512]{1,0:T(8,128)}, f32[448,512]{1,0:T(8,128)}, f32[448,512]{1,0:T(8,128)}, f32[12,512]{1,0:T(8,128)}) custom-call(f32[256,512]{1,0:T(8,128)} %get-tuple-element.15.refs_0_, f32[448,512]{1,0:T(8,128)} %get-tuple-element.16.refs_1_, f32[448,512]{1,0:T(8,128)} %get-tuple-element.17.refs_2_, ...), custom_call_target="tpu_custom_call" | custom-call | tf_op jit(solution)/shard_map/finish/pallas_call | solution.py:614

commit v4 on v3

--- a/solution.py
+++ b/solution.py
@@ -113,7 +113,7 @@
 
     def tp_ag_start(ph, buf, at):
         mine = buf.at[at(z, xh, c)]
-        loop(1, N, lambda k: rdma(mine, mine, tp_ss.at[ph, k], tp_rs.at[ph, k], tp_to(k)).start())
+        each(N_FAR[::-1], lambda k: rdma(mine, mine, tp_ss.at[ph, k], tp_rs.at[ph, k], tp_to(k)).start())
         rdma(mine, mine, fw_ss.at[ph, 0], fw_rs.at[ph, 0], other).start()
         late.append(
             lambda: loop(
@@ -329,7 +329,7 @@
     def at_g(i):
         return (i,)
 
-    grp_ag_start(1, h, at_g, range(1, G))
+    grp_ag_start(1, h, at_g, G_ORDER[1:])
     if pairs[cut:]:
         lagged(pairs[cut:], t_arrive, t_use)
     grp_sent(2, t2s, t2r)
@@ -491,7 +491,7 @@
     lane = lax.broadcasted_iota(jnp.int32, gate_grad.shape, 1)
     gu[g, :, 2 * A :] = jnp.where(lane < B, gate_grad, pltpu.roll(up_grad, B, 1)).astype(BF)
 
-    grp_ag_start(7, gu, at_g, range(1, G))
+    grp_ag_start(7, gu, at_g, G_ORDER[1:])
 
     def s10_first(k):
         i = grp_arrived(7, gu, k)

time: 146 us -> 142 us (0.973)
  Pallas kernels: 143 us -> 139 us
    pallas_call x1, Pallas kernels: 140 us -> 136 us  [body(): pl.pallas_call(functools.partial(kernel, sizes), out_shape=(S((G * off, d...]
where the time goes in v4:
time: 142 us; the launch traced here: 139 us
  Pallas kernels  139 us (98%)
    pallas_call x1, Pallas kernels, body(): pl.pallas_call(functools.partial(kernel, sizes), out_shape=(S((G * off, d...  136 us
    pallas_call x1, Pallas kernels, body(): pl.pallas_call(finish, out_shape=tuple((S(*shape) for shape in shapes)),...  2.96 us

profile of v4, /device:TPU:53, one launch (start us, length us, event | category | flops | bytes accessed | tf_op | source)
XLA Modules:
  0.0 139.3 jit_solution(1060863789697848005)
XLA Ops:
  0.6 135.7 %chain.1 = (f32[256,512]{1,0:T(8,128)}, f32[448,512]{1,0:T(8,128)}, f32[448,512]{1,0:T(8,128)}, f32[448,512]{1,0:T(8,128)}, f32[12,512]{1,0:T(8,128)}) custom-call(bf16[12,1024]{1,0:T(8,128)(2,1)} %t_in.1, bf16[1024,896]{1,0:T(8,128)(2,1)} %t_gate.1, bf16[1024,896]{1,0:T(8,128)(2,1)} %t_up.1, bf16[896,1024]{1,0:T(8,128)(2,1)} %t_down.1, ...), custom_call_target="tpu_custom_call" | custom-call | tf_op jit(solution)/shard_map/chain/pallas_call | solution.py:597
  136.3 3.0 %finish.1 = (f32[256,512]{1,0:T(8,128)}, f32[448,512]{1,0:T(8,128)}, f32[448,512]{1,0:T(8,128)}, f32[448,512]{1,0:T(8,128)}, f32[12,512]{1,0:T(8,128)}) custom-call(f32[256,512]{1,0:T(8,128)} %get-tuple-element.15.refs_0_, f32[448,512]{1,0:T(8,128)} %get-tuple-element.16.refs_1_, f32[448,512]{1,0:T(8,128)} %get-tuple-element.17.refs_2_, ...), custom_call_target="tpu_custom_call" | custom-call | tf_op jit(solution)/shard_map/finish/pallas_call | solution.py:614
